TPU v7x, 32 devices: a whole 2x2x4 slice. The times are simulated.
32 devices in a mesh: dp: 2 (over x), tp: 4 (over z), sp: 4 (over y, core).
Axes of the slice: x: 2, y: 2, z: 4, core: 2. Of those that a mesh axis runs over, the one named last changes fastest.
Arguments:
- hidden: bfloat16 [64, 4096], P('dp'), parts along dimension 0
- positions: int32 [64], P('dp'), parts along dimension 0
- k_cache: bfloat16 [64, 32, 512, 128], P('dp', 'tp', 'sp'), parts along dimension 0
- v_cache: bfloat16 [64, 32, 512, 128], P('dp', 'tp', 'sp'), parts along dimension 0
- ln1_gain: bfloat16 [4096], replicated
- ln1_bias: bfloat16 [4096], replicated
- w_query: bfloat16 [4096, 4096], P(None, 'tp')
- b_query: bfloat16 [4096], P('tp')
- w_key: bfloat16 [4096, 4096], P(None, 'tp')
- b_key: bfloat16 [4096], P('tp')
- w_value: bfloat16 [4096, 4096], P(None, 'tp')
- b_value: bfloat16 [4096], P('tp')
- w_out: bfloat16 [4096, 4096], P('tp')
- b_out: bfloat16 [4096], replicated
- ln2_gain: bfloat16 [4096], replicated
- ln2_bias: bfloat16 [4096], replicated
- w_fc1: bfloat16 [4096, 16384], P(None, 'tp')
- b_fc1: bfloat16 [16384], P('tp')
- w_fc2: bfloat16 [16384, 4096], P('tp')
- b_fc2: bfloat16 [4096], replicated
Outputs:
- output 1: bfloat16 [64, 4096], P('dp'), parts along dimension 0
- output 2: bfloat16 [64, 32, 512, 128], P('dp', 'tp', 'sp'), parts along dimension 0
- output 3: bfloat16 [64, 32, 512, 128], P('dp', 'tp', 'sp'), parts along dimension 0
There are 2 independent parts. A program takes and returns all parts, laid end to end along the dimension named above; an argument that names none is the same for every part.
All inputs are finite; a program needn't handle non-finite values.
Results may differ from a plain program's by a relative error of at most 0.0078411.
Values sent between devices are 32-bit elements.
A program may use at most 1 GiB of HBM per device.

v0:
```python
import jax
import jax.numpy as jnp
from jax import lax
from jax.sharding import PartitionSpec as P

LN_EPS = 1e-5


def layer_norm(values, ln_gain, ln_bias):
    as_f32 = values.astype(jnp.float32)
    centered = as_f32 - as_f32.mean(-1, keepdims=True)
    variance = (centered * centered).mean(-1, keepdims=True)
    return (centered * lax.rsqrt(variance + LN_EPS) * ln_gain.astype(jnp.float32) + ln_bias.astype(jnp.float32)).astype(jnp.bfloat16)


def project(normed, weight, bias_vec):
    return jnp.dot(normed, weight, preferred_element_type=jnp.float32) + bias_vec.astype(jnp.float32)


def finish_layer(hidden, attn_vec, w_out, b_out, ln2_gain, ln2_bias, w_fc1, b_fc1, w_fc2, b_fc2):
    attn_part = jnp.dot(attn_vec, w_out, preferred_element_type=jnp.float32)
    attn_sum = lax.psum(attn_part, 'tp')
    resid_one = (hidden.astype(jnp.float32) + attn_sum + b_out.astype(jnp.float32)).astype(jnp.bfloat16)
    normed_two = layer_norm(resid_one, ln2_gain, ln2_bias)
    activated = jax.nn.relu(project(normed_two, w_fc1, b_fc1)).astype(jnp.bfloat16)
    mlp_part = jnp.dot(activated, w_fc2, preferred_element_type=jnp.float32)
    mlp_sum = lax.psum(mlp_part, 'tp')
    return (resid_one.astype(jnp.float32) + mlp_sum + b_fc2.astype(jnp.float32)).astype(jnp.bfloat16)


def solution(mesh):
    cache_spec = P('dp', 'tp', 'sp', None)
    col_spec = P(None, 'tp')
    row_spec = P('tp', None)
    in_specs = (P('dp', None), P('dp'), cache_spec, cache_spec, P(), P(), col_spec, P('tp'), col_spec, P('tp'),
                col_spec, P('tp'), row_spec, P(), P(), P(), col_spec, P('tp'), row_spec, P())
    out_specs = (P('dp', None), cache_spec, cache_spec)

    def local_layer(hidden, positions, k_cache, v_cache, ln1_gain, ln1_bias, w_query, b_query, w_key, b_key, w_value, b_value, w_out, b_out, ln2_gain, ln2_bias, w_fc1, b_fc1, w_fc2, b_fc2):
        n_batch, heads_loc, block_len, head_dim = k_cache.shape
        head_shape = (n_batch, heads_loc, head_dim)
        normed = layer_norm(hidden, ln1_gain, ln1_bias)
        query_vec = (project(normed, w_query, b_query) * head_dim ** -0.5).astype(jnp.bfloat16).reshape(head_shape)
        new_key = project(normed, w_key, b_key).astype(jnp.bfloat16).reshape(head_shape)
        new_value = project(normed, w_value, b_value).astype(jnp.bfloat16).reshape(head_shape)
        local_pos = positions - lax.axis_index('sp') * block_len
        slot_ids = jnp.arange(block_len)
        at_slot = (slot_ids[None, :] == local_pos[:, None])[:, None, :, None]
        k_next = jnp.where(at_slot, new_key[:, :, None, :], k_cache)
        v_next = jnp.where(at_slot, new_value[:, :, None, :], v_cache)
        valid_mask = (slot_ids[None, :] <= local_pos[:, None])[:, None, :]
        scores = jnp.einsum('bhd,bhsd->bhs', query_vec, k_next, preferred_element_type=jnp.float32)
        scores = jnp.where(valid_mask, scores, -1e30)
        block_max = scores.max(-1)
        weights = jnp.where(valid_mask, jnp.exp(scores - block_max[..., None]), 0.0)
        block_sum = weights.sum(-1)
        block_out = jnp.einsum('bhs,bhsd->bhd', weights.astype(jnp.bfloat16), v_next, preferred_element_type=jnp.float32)
        block_stats = jnp.concatenate([block_out, block_max[..., None], block_sum[..., None]], axis=-1)
        gathered = lax.all_gather(block_stats, 'sp')
        maxima = gathered[..., head_dim]
        factors = jnp.exp(maxima - maxima.max(0))
        denom_sum = (factors * gathered[..., head_dim + 1]).sum(0)
        mixed_out = (factors[..., None] * gathered[..., :head_dim]).sum(0) / denom_sum[..., None]
        attn_vec = mixed_out.astype(jnp.bfloat16).reshape(n_batch, heads_loc * head_dim)
        result = finish_layer(hidden, attn_vec, w_out, b_out, ln2_gain, ln2_bias, w_fc1, b_fc1, w_fc2, b_fc2)
        return result, k_next, v_next

    return jax.shard_map(local_layer, mesh=mesh, in_specs=in_specs, out_specs=out_specs, check_vma=False)
```

profile of v0, /device:TPU:0, one launch (start us, length us, event | category | flops | bytes accessed | tf_op | source)
XLA Modules:
  0.0 180.2 jit_solution(1612317083605994457)
XLA Ops:
  7.2 1.2 convert_reduce_fusion.1
  8.5 1.8 %fusion.17 = f32[32]{0:T(128)S(1)} fusion(bf16[32,4096]{1,0:T(8,128)(2,1)} %param.20, f32[32]{0:T(128)S(1)} %broadcast_multiply_fusion.1), kind=kLoop, calls=%fused_computation.29 | loop fusion | flops 524256 | bytes 262400 | tf_op jit(solution)/shard_map/reduce_sum | solution.py:12
  10.3 0.7 convert_element_type.73
  11.0 0.7 convert_element_type.74
  11.7 0.7 convert_element_type.78
  12.4 5.1 %fusion.8 = bf16[4,8,8,128]{3,1,2,0:T(8,128)(2,1)S(1)} fusion(bf16[4096,1024]{1,0:T(8,128)(2,1)} %param.28, f32[1024]{0:T(1024)S(1)} %convert_element_type.78, bf16[32,4096]{1,0:T(8,128)(2,1)} %param.20, f32[4096]{0:T(1024)S(1)} %convert_element_type.74, f32[4096]{0:T(1024)S(1)} %convert_element_type.73, f32[32]{0:T(128)S(1)} %add_rsqrt_fusion.1, ...), kind=kOutput, calls=%fused_computation.14 | convolution fusion | flops 269287424 | bytes 8753408 | tf_op jit(solution)/shard_map/dot_general | solution.py:17
  17.6 1.6 fusion.7
  19.4 5.0 %fusion.4 = bf16[32,1024]{1,0:T(8,128)(2,1)S(1)} fusion(bf16[4096,1024]{1,0:T(8,128)(2,1)} %param.26, f32[1024]{0:T(1024)S(1)} %convert_element_type.76, bf16[32,4096]{1,0:T(8,128)(2,1)S(1)} %copy-done.1, f32[4096]{0:T(1024)S(1)} %convert_element_type.74, f32[4096]{0:T(1024)S(1)} %convert_element_type.73, f32[32]{0:T(128)S(1)} %add_rsqrt_fusion.1, ...), kind=kOutput, calls=%fused_computation.10 | convolution fusion | flops 269320192 | bytes 8753408 | tf_op jit(solution)/shard_map/dot_general | solution.py:17
  24.4 9.3 %broadcast_select_fusion = (bf16[32,8,128,128]{3,2,1,0:T(8,128)(2,1)}, bf16[32,8,128,128]{3,2,1,0:T(8,128)(2,1)S(1)}) fusion(bf16[32,8,128,128]{3,2,1,0:T(8,128)(2,1)} %param.23, pred[32,128]{1,0:T(8,128)(4,1)S(1)} %get-tuple-element.13, bf16[32,8,128]{2,1,0:T(8,128)(2,1)S(1)} %bitcast.47, bf16[32,8,128,128]{3,2,1,0:T(8,128)(2,1)} %param.22, ...), kind=kLoop, calls=%fused_computation | loop fusion | flops 8388608 | bytes 33689600 | tf_op jit(solution)/shard_map/jit(_where)/select_n | solution.py:50
  33.7 3.4 %copy-done = bf16[32,8,128,128]{3,2,1,0:T(8,128)(2,1)} copy-done((bf16[32,8,128,128]{3,2,1,0:T(8,128)(2,1)}, bf16[32,8,128,128]{3,2,1,0:T(8,128)(2,1)S(1)}, u32[]{:S(2)}) %copy-start) | copy-done | bytes 8388632
  37.1 4.4 %fusion.54 = f32[32,8,1,128]{3,2,1,0:T(1,128)S(1)} fusion(bf16[32,8,128,1]{2,3,1,0:T(2,128)(2,1)S(1)} %reshape.95, bf16[32,8,128,128]{3,2,1,0:T(8,128)(2,1)S(1)} %get-tuple-element.11), kind=kOutput, calls=%fused_computation.72 | convolution fusion | flops 8388608 | bytes 8585216 | tf_op jit(solution)/shard_map/bhd,bhsd->bhs/dot_general | solution.py:52
  41.5 0.1 select_reduce_fusion
  41.6 0.2 fusion.42
  41.8 0.3 copy.60
  42.1 0.3 copy.59
  42.4 5.6 %fusion.38 = f32[32,8,1,128]{3,2,1,0:T(1,128)S(1)} fusion(bf16[32,8,128,128]{3,2,1,0:T(8,128)(2,1)} %get-tuple-element.10, bf16[32,8,128,1]{2,1,0,3:T(8,128)(2,1)S(1)} %get-tuple-element.8), kind=kOutput, calls=%fused_computation.46 | convolution fusion | flops 8388608 | bytes 8585216 | tf_op jit(solution)/shard_map/bhs,bhsd->bhd/dot_general | solution.py:57
  48.0 0.1 pad_maximum_fusion
  48.1 11.6 %all-gather = f32[128,8,130]{2,1,0:T(8,128)S(1)} all-gather(f32[32,8,130]{2,1,0:T(8,128)S(1)} %pad_maximum_fusion), channel_id=2, replica_groups=mesh['dp'=2,'tp'=4,'sp'=4] {'sp'}, dimensions={0}, use_global_device_ids=true | all-gather | bytes 665600 | tf_op jit(solution)/shard_map/all_gather | solution.py:59
  59.7 0.3 fusion.53
  60.0 0.3 copy.63
  60.2 0.3 copy.73
  60.6 0.1 copy.64
  60.8 0.2 fusion.25
  61.0 0.1 divide_convert_fusion
  61.1 5.7 %fusion.43 = f32[32,4096]{1,0:T(8,128)} fusion(bf16[1024,4096]{1,0:T(8,128)(2,1)} %param.32, bf16[4,8,8,128]{3,2,1,0:T(8,128)(2,1)S(1)} %bitcast.45), kind=kOutput, calls=%fused_computation.54 | convolution fusion | flops 268435456 | bytes 8978432 | tf_op jit(solution)/shard_map/dot_general | solution.py:21
  66.9 0.2 all-reduce.5.cloned.1.call-start
  67.2 39.3 %all-reduce.3.cloned.1.call-done = f32[32,4096]{1,0:T(8,128)} async-done(((f32[32,4096]{1,0:T(8,128)}), f32[32,4096]{1,0:T(8,128)}) %all-reduce.3.cloned.1.call-update) | async-done | bytes 524304 | tf_op jit(solution)/shard_map/psum | solution.py:22
  106.5 1.2 convert_reduce_fusion
  107.7 0.3 fusion.13
  108.0 25.1 %fusion.2 = f32[32,4096]{1,0:T(8,128)} fusion(bf16[4096,4096]{1,0:T(8,128)(2,1)} %param.38, bf16[4096,4096]{1,0:T(8,128)(2,1)} %param.36, bf16[32,4096]{1,0:T(8,128)(2,1)S(1)} %get-tuple-element.4, f32[4096]{0:T(1024)S(1)} %convert_element_type.91, f32[4096]{0:T(1024)S(1)} %convert_element_type.89, f32[4096]{0:T(1024)S(1)} %convert_element_type.88, ...), kind=kOutput, calls=%fused_computation.5 | convolution fusion | flops 2148663296 | bytes 67944704 | tf_op jit(solution)/shard_map/dot_general | solution.py:26
  133.2 38.4 %all-reduce.5.cloned.1.call-done = f32[32,4096]{1,0:T(8,128)} async-done(((f32[32,4096]{1,0:T(8,128)}), f32[32,4096]{1,0:T(8,128)}) %all-reduce.5.cloned.1.call-update) | async-done | bytes 524304 | tf_op jit(solution)/shard_map/psum | solution.py:27
  171.6 1.8 %fusion.24 = bf16[32,4096]{1,0:T(8,128)(2,1)} fusion(f32[32,4096]{1,0:T(8,128)} %all-reduce.5.cloned.1.call-done, bf16[32,4096]{1,0:T(8,128)(2,1)S(1)} %get-tuple-element.4, f32[4096]{0:T(1024)S(1)} %convert_element_type.93), kind=kLoop, calls=%fused_computation.36 | loop fusion | flops 524288 | bytes 1064960 | tf_op jit(solution)/shard_map/convert_element_type | solution.py:28
  (44 shorter events, 0.5 us)
Async XLA Ops:
  7.2 10.4 %copy-start.1 = (bf16[32,4096]{1,0:T(8,128)(2,1)S(1)}, bf16[32,4096]{1,0:T(8,128)(2,1)}, u32[]{:S(2)}) copy-start(bf16[32,4096]{1,0:T(8,128)(2,1)} %param.20) | copy-start | bytes 786436
  7.2 10.4 %copy-start.8 = (bf16[1024]{0:T(1024)(128)(2,1)S(1)}, bf16[1024]{0:T(1024)(128)(2,1)}, u32[]{:S(2)}) copy-start(bf16[1024]{0:T(1024)(128)(2,1)} %param.31) | copy-start | bytes 6148
  7.2 99.3 %all-reduce.3.cloned.1.call-start = ((), (), s32[]{:S(2)}) async-start(), calls=%async_computation | async-start | bytes 1048576 | tf_op jit(solution)/shard_map/psum | solution.py:22
  7.2 10.4 %copy-start.2 = (bf16[4096,1024]{1,0:T(8,128)(2,1)S(1)}, bf16[4096,1024]{1,0:T(8,128)(2,1)}, u32[]{:S(2)}) copy-start(bf16[4096,1024]{1,0:T(8,128)(2,1)} %param.30) | copy-start | bytes 25165828
  12.4 6.8 %copy-start.10 = (s32[32]{0:T(128)S(1)}, s32[32]{0:T(128)}, u32[]{:S(2)}) copy-start(s32[32]{0:T(128)} %param.21) | copy-start | bytes 388
  12.4 6.9 %copy-start.9 = (bf16[1024]{0:T(1024)(128)(2,1)S(1)}, bf16[1024]{0:T(1024)(128)(2,1)}, u32[]{:S(2)}) copy-start(bf16[1024]{0:T(1024)(128)(2,1)} %param.27) | copy-start | bytes 6148
  33.7 3.4 %copy-start = (bf16[32,8,128,128]{3,2,1,0:T(8,128)(2,1)}, bf16[32,8,128,128]{3,2,1,0:T(8,128)(2,1)S(1)}, u32[]{:S(2)}) copy-start(bf16[32,8,128,128]{3,2,1,0:T(8,128)(2,1)S(1)} %get-tuple-element.11) | copy-start | bytes 25165828
  60.8 6.4 %copy-start.3 = (bf16[4096]{0:T(1024)(128)(2,1)S(1)}, bf16[4096]{0:T(1024)(128)(2,1)}, u32[]{:S(2)}) copy-start(bf16[4096]{0:T(1024)(128)(2,1)} %param.33) | copy-start | bytes 24580
  60.8 6.4 %copy-start.4 = (bf16[4096]{0:T(1024)(128)(2,1)S(1)}, bf16[4096]{0:T(1024)(128)(2,1)}, u32[]{:S(2)}) copy-start(bf16[4096]{0:T(1024)(128)(2,1)} %param.34) | copy-start | bytes 24580
  60.8 6.4 %copy-start.5 = (bf16[4096]{0:T(1024)(128)(2,1)S(1)}, bf16[4096]{0:T(1024)(128)(2,1)}, u32[]{:S(2)}) copy-start(bf16[4096]{0:T(1024)(128)(2,1)} %param.35) | copy-start | bytes 24580
  60.8 6.4 %copy-start.6 = (bf16[4096]{0:T(1024)(128)(2,1)S(1)}, bf16[4096]{0:T(1024)(128)(2,1)}, u32[]{:S(2)}) copy-start(bf16[4096]{0:T(1024)(128)(2,1)} %param.37) | copy-start | bytes 24580
  66.9 104.7 %all-reduce.5.cloned.1.call-start = ((), (), s32[]{:S(2)}) async-start(), calls=%async_computation.1 | async-start | bytes 1048576 | tf_op jit(solution)/shard_map/psum | solution.py:27
  108.0 25.2 %copy-start.7 = (bf16[4096]{0:T(1024)(128)(2,1)S(1)}, bf16[4096]{0:T(1024)(128)(2,1)}, u32[]{:S(2)}) copy-start(bf16[4096]{0:T(1024)(128)(2,1)} %param.39) | copy-start | bytes 24580
Sparse Core Ops, SparseCore 0:
  67.0 39.4 all-reduce.2
  133.3 38.2 all-reduce.4
where the time goes:
time: 181 us; the launch traced here: 180 us
  waiting for transfers between devices  77.7 us (43%)
  matrix products  52.7 us (29%)
  other arithmetic  18.9 us (10%)
  between operations  14.4 us (8%)
  blocking collectives  11.6 us (6%)
  local copies, waits for them, and re-layouts  4.81 us (3%)
    psum x1, waiting for transfers between devices, finish_layer(): attn_sum = lax.psum(attn_part, 'tp')  39.3 us
    psum x1, waiting for transfers between devices, finish_layer(): mlp_sum = lax.psum(mlp_part, 'tp')  38.4 us
    dot_general x1, matrix products, finish_layer(): mlp_part = jnp.dot(activated, w_fc2, preferred_element_type=jnp.float32)  25.1 us
    dot_general x3, matrix products, project(): jnp.dot(normed, weight, preferred_element_type=jnp.float32)  11.7 us
    all_gather x1, blocking collectives, local_layer(): gathered = lax.all_gather(block_stats, 'sp')  11.6 us
    select_n x1, other arithmetic, local_layer(): v_next = jnp.where(at_slot, new_value[:, :, None, :], v_cache)  9.27 us
    dot_general x1, matrix products, finish_layer(): attn_part = jnp.dot(attn_vec, w_out, preferred_element_type=jnp.float32)  5.74 us
    dot_general x1, matrix products, local_layer(): jnp.einsum('bhs,bhsd->bhd', weights.astype(jnp.bfloat16), v_next, preferr...  5.65 us
  transfers between devices with their start and end apart: 2, of which 2 were waited for; matrix products, arithmetic and copies ran while one was open for 0% of the time, Pallas kernels for 0%

commit v1 on v0

v1 whole, which is shorter than its diff:
```python
import jax
import jax.numpy as jnp
from jax import lax
from jax.experimental import pallas as pl
from jax.experimental.pallas import tpu as pltpu
from jax.sharding import PartitionSpec as P

LN_EPS = 1e-5
NEG = -1e30
F32 = jnp.float32
BF16 = jnp.bfloat16
MESH = pl.DeviceIdType.MESH
ROWS = 32
HALF_ROWS = 16
DIM = 4096
HEADS = 8
HEAD_DIM = 128
BLOCK_LEN = 128
MIB = 1 << 20


def any_spec():
    return pl.BlockSpec(memory_space=pltpu.HBM)


def vmem_spec():
    return pl.BlockSpec(memory_space=pltpu.VMEM)


def remote(src, dst, send_sem, recv_sem, device):
    return pltpu.make_async_remote_copy(src_ref=src, dst_ref=dst, send_sem=send_sem, recv_sem=recv_sem,
                                        device_id=device, device_id_type=MESH)


def dyn(start, size):
    return pl.ds(pl.multiple_of(start, size), size)


QKV_CHUNKS = 4
QKV_ROWS = DIM // QKV_CHUNKS


def as_row(vec_ref):
    return vec_ref[...].astype(F32)[None, :]


def qkv_kernel(h_hbm, g_hbm, b_hbm, wq_ref, wk_ref, wv_ref, bq_hbm, bk_hbm, bv_hbm, out_ref,
               h_buf, g_buf, b_buf, bq_buf, bk_buf, bv_buf, bias_rows, wbuf, norm, send, recv, vsem, wsem, ssem, rsem):
    smalls = [pltpu.make_async_copy(src, dst, vsem.at[n]) for n, (src, dst) in enumerate((
        (h_hbm, h_buf), (g_hbm, g_buf), (b_hbm, b_buf), (bq_hbm, bq_buf), (bk_hbm, bk_buf), (bv_hbm, bv_buf)))]
    for copy in smalls:
        copy.start()
    sp = lax.axis_index('sp')
    core = lax.rem(sp, 2)
    partner = sp + 1 - 2 * core
    cols = dyn(core * 512, 512)
    copies = []
    for i, weight in enumerate((wq_ref, wk_ref, wv_ref)):
        for j in range(QKV_CHUNKS):
            rows = pl.ds(j * QKV_ROWS, QKV_ROWS)
            copy = pltpu.make_async_copy(weight.at[rows, cols], wbuf.at[i, rows, :], wsem.at[i, j])
            copy.start()
            copies.append(copy)
    barrier = pltpu.get_barrier_semaphore()
    pl.semaphore_signal(barrier, inc=1, device_id={'sp': partner}, device_id_type=MESH)

    for copy in smalls:
        copy.wait()
    values = h_buf[...].astype(F32)
    centered = values - jnp.mean(values, -1, keepdims=True)
    variance = jnp.mean(centered * centered, -1, keepdims=True)
    norm[...] = (centered * lax.rsqrt(variance + LN_EPS) * as_row(g_buf) + as_row(b_buf)).astype(BF16)
    for i, buf in enumerate((bq_buf, bk_buf, bv_buf)):
        bias_rows[i] = as_row(buf)

    pl.semaphore_wait(barrier, 1)
    sends = []
    for i in range(3):
        total = None
        for j in range(QKV_CHUNKS):
            copies[i * QKV_CHUNKS + j].wait()
            rows = pl.ds(j * QKV_ROWS, QKV_ROWS)
            part = jnp.dot(norm[:, rows], wbuf[i, rows, :], preferred_element_type=F32)
            total = part if total is None else total + part
        total = total + bias_rows[i, :, cols]
        if i == 0:
            total = total * HEAD_DIM ** -0.5
        total = total.astype(BF16).astype(F32)
        for h in range(4):
            send[i, h] = total[:, h * 128:(h + 1) * 128]
        copy = remote(send.at[i], recv.at[i], ssem.at[i], rsem.at[i], {'sp': partner})
        copy.start()
        sends.append(copy)
        for h in range(4):
            out_ref[i, core * 4 + h] = total[:, h * 128:(h + 1) * 128]
    for i in range(3):
        sends[i].wait_recv()
        for h in range(4):
            out_ref[i, (1 - core) * 4 + h] = recv[i, h]
    for i in range(3):
        sends[i].wait_send()


def qkv_call(hidden, gain, bias, w_query, b_query, w_key, b_key, w_value, b_value):
    return pl.pallas_call(
        qkv_kernel,
        out_shape=jax.ShapeDtypeStruct((3, HEADS, ROWS, HEAD_DIM), F32),
        in_specs=[any_spec()] * 9,
        out_specs=vmem_spec(),
        scratch_shapes=[
            pltpu.VMEM((ROWS, DIM), BF16),
            pltpu.VMEM((DIM,), BF16), pltpu.VMEM((DIM,), BF16),
            pltpu.VMEM((1024,), BF16), pltpu.VMEM((1024,), BF16), pltpu.VMEM((1024,), BF16),
            pltpu.VMEM((3, 1, 1024), F32),
            pltpu.VMEM((3, DIM, 512), BF16),
            pltpu.VMEM((ROWS, DIM), BF16),
            pltpu.VMEM((3, 4, ROWS, 128), F32),
            pltpu.VMEM((3, 4, ROWS, 128), F32),
            pltpu.SemaphoreType.DMA((6,)),
            pltpu.SemaphoreType.DMA((3, QKV_CHUNKS)),
            pltpu.SemaphoreType.DMA((3,)),
            pltpu.SemaphoreType.DMA((3,)),
        ],
        compiler_params=pltpu.CompilerParams(collective_id=0, has_side_effects=True, vmem_limit_bytes=24 * MIB),
        name='qkv',
    )(hidden, gain, bias, w_query, w_key, w_value, b_query, b_key, b_value)


CHUNK = 4
NUM_CHUNKS = ROWS // CHUNK


def attn_kernel(pos_ref, qkv_ref, k_hbm, v_hbm, k_out, v_out, o_ref, st_ref, kbuf, vbuf, qs, kin, vin, kdone, vdone):
    base = lax.axis_index('sp') * BLOCK_LEN

    def chunk_copy(src, dst, sem, p):
        rows = pl.ds(p * CHUNK, CHUNK)
        return pltpu.make_async_copy(src.at[rows], dst.at[rows], sem.at[p])

    for p in range(NUM_CHUNKS):
        chunk_copy(k_hbm, kbuf, kin, p).start()
        chunk_copy(v_hbm, vbuf, vin, p).start()
    for i in range(3):
        qs[i] = jnp.swapaxes(qkv_ref[i], 0, 1)

    row = lax.broadcasted_iota(jnp.int32, (16, 128), 0)
    lane = lax.broadcasted_iota(jnp.int32, (16, 128), 1)
    head_of_row = lax.rem(row, 8)
    first = row < 8
    lane8 = lax.broadcasted_iota(jnp.int32, (8, 128), 1)

    def patch(buf, b, local, new):
        start = pl.multiple_of((local // 16) * 16, 16)
        tile = buf[b, :, pl.ds(start, 16), :].astype(F32)
        slot = lax.broadcasted_iota(jnp.int32, (8, 16, 128), 1)
        buf[b, :, pl.ds(start, 16), :] = jnp.where(slot == local - start, new[:, None, :], tile).astype(BF16)

    def spread(values, j):
        return jnp.concatenate([jnp.where(head_of_row == 2 * j, values, 0.0),
                                jnp.where(head_of_row == 2 * j + 1, values, 0.0)], axis=1).astype(BF16)

    def body(p, carry):
        mm, ll = carry
        chunk_copy(k_hbm, kbuf, kin, p).wait()
        chunk_copy(v_hbm, vbuf, vin, p).wait()
        locals_ = [pos_ref[p * CHUNK + t] - base for t in range(CHUNK)]
        for t in range(CHUNK):
            b = p * CHUNK + t
            local = locals_[t]

            @pl.when((local >= 0) & (local < BLOCK_LEN))
            def _():
                patch(kbuf, b, local, qs[1, b])
                patch(vbuf, b, local, qs[2, b])

        chunk_copy(kbuf, k_out, kdone, p).start()
        chunk_copy(vbuf, v_out, vdone, p).start()

        scores = []
        for t in range(0, CHUNK, 2):
            b = p * CHUNK + t
            query = qs[0, pl.ds(b, 2)].reshape(16, 128)
            total = None
            for j in range(4):
                keys = jnp.concatenate([jnp.concatenate([kbuf[b + e, 2 * j], kbuf[b + e, 2 * j + 1]], axis=1)
                                        for e in range(2)], axis=0)
                part = lax.dot_general(spread(query, j), keys, (((1,), (1,)), ((), ())), preferred_element_type=F32)
                total = part if total is None else total + part
            scores.append(jnp.where(first, total[:, :128], total[:, 128:]))
        weights = []
        for n, t in enumerate(range(0, CHUNK, 2)):
            b = p * CHUNK + t
            valid = lane <= jnp.where(first, locals_[t], locals_[t + 1])
            masked = jnp.where(valid, scores[n], NEG)
            top = masked.max(-1, keepdims=True)
            weight = jnp.where(valid, jnp.exp(masked - top), 0.0)
            denom = weight.sum(-1, keepdims=True)
            weights.append(weight)
            for e in range(2):
                mm = jnp.where(lane8 == b + e, top[8 * e:8 * e + 8], mm)
                ll = jnp.where(lane8 == b + e, denom[8 * e:8 * e + 8], ll)
        for n, t in enumerate(range(0, CHUNK, 2)):
            b = p * CHUNK + t
            total = None
            for j in range(4):
                vals = jnp.concatenate([vbuf[b + e, 2 * j:2 * j + 2].reshape(256, 128) for e in range(2)], axis=1)
                part = jnp.dot(spread(weights[n], j), vals, preferred_element_type=F32)
                total = part if total is None else total + part
            o_ref[pl.ds(b, 2)] = jnp.where(first, total[:, :128], total[:, 128:]).reshape(2, 8, 128)
        return mm, ll

    zeros = jnp.zeros((8, 128), F32)
    mm, ll = lax.fori_loop(0, NUM_CHUNKS, body, (zeros, zeros))
    st_ref[0] = mm
    st_ref[1] = ll
    for p in range(NUM_CHUNKS):
        chunk_copy(kbuf, k_out, kdone, p).wait()
        chunk_copy(vbuf, v_out, vdone, p).wait()


def attn_call(positions, qkv, k_cache, v_cache):
    cache = jax.ShapeDtypeStruct(k_cache.shape, BF16)
    return pl.pallas_call(
        attn_kernel,
        out_shape=(cache, cache, jax.ShapeDtypeStruct((ROWS, HEADS, HEAD_DIM), F32),
                   jax.ShapeDtypeStruct((2, HEADS, 128), F32)),
        in_specs=[pl.BlockSpec(memory_space=pltpu.SMEM), vmem_spec(), any_spec(), any_spec()],
        out_specs=(any_spec(), any_spec(), vmem_spec(), vmem_spec()),
        scratch_shapes=[
            pltpu.VMEM(k_cache.shape, BF16),
            pltpu.VMEM(k_cache.shape, BF16),
            pltpu.VMEM((3, ROWS, HEADS, HEAD_DIM), F32),
            pltpu.SemaphoreType.DMA((NUM_CHUNKS,)),
            pltpu.SemaphoreType.DMA((NUM_CHUNKS,)),
            pltpu.SemaphoreType.DMA((NUM_CHUNKS,)),
            pltpu.SemaphoreType.DMA((NUM_CHUNKS,)),
        ],
        compiler_params=pltpu.CompilerParams(vmem_limit_bytes=24 * MIB),
        name='attn',
    )(positions, qkv, k_cache, v_cache)


SEND_ORDER = (3, 2, 1)


def finish_kernel(o_ref, st_ref, hid_hbm, bo_hbm, g_hbm, b_hbm, b1_hbm, b2_hbm, wo_hbm, w1_hbm, w2_hbm, out_ref,
                  hid_ref, bo_buf, g_buf, b_buf, b1_buf, b2_buf, rows_ref, small_sem,
                  wo_buf, w1_buf, w2_buf, c1_o, c1_s, cs_o, cs_s, c2_o, c2_s, a_f32, a_bf, rs_send, rs_recv,
                  m_own, m_send, m_recv, gat, y_bf, u_bf,
                  wo_sem, w1_sem, w2_sem, c_ssem, c_rsem, rs_ssem, rs_rsem, m_ssem, m_rsem, g_ssem, g_rsem):
    z = lax.axis_index('tp')
    sp = lax.axis_index('sp')
    core = lax.rem(sp, 2)
    yy = sp // 2
    partner = sp + 1 - 2 * core
    across = lax.rem(sp + 2, 4)
    across_other = lax.rem(partner + 2, 4)
    zpeer = {1: z + 1 - 2 * lax.rem(z, 2), 2: lax.rem(z + 2, 4), 3: 3 - z, 0: z}

    smalls = [pltpu.make_async_copy(src, dst, small_sem.at[n]) for n, (src, dst) in enumerate((
        (hid_hbm, hid_ref), (bo_hbm, bo_buf), (g_hbm, g_buf), (b_hbm, b_buf), (b1_hbm, b1_buf), (b2_hbm, b2_buf)))]
    for copy in smalls:
        copy.start()
    loads = []
    for j in range(4):
        loads.append(pltpu.make_async_copy(wo_hbm.at[:, dyn(yy * 2048 + j * 512, 512)], wo_buf.at[j], wo_sem.at[j]))
    for j in range(4):
        loads.append(pltpu.make_async_copy(w1_hbm.at[:, dyn(core * 2048 + j * 512, 512)], w1_buf.at[j], w1_sem.at[j]))
    for j in range(4):
        loads.append(pltpu.make_async_copy(w2_hbm.at[dyn(core * 2048, 2048), dyn(yy * 2048 + j * 512, 512)],
                                           w2_buf.at[j], w2_sem.at[j]))
    for load in loads:
        load.start()

    barrier = pltpu.get_barrier_semaphore()
    for k in (1, 2, 3):
        pl.semaphore_signal(barrier, inc=1, device_id={'tp': zpeer[k]}, device_id_type=MESH)
    for peer in (partner, across, across_other):
        pl.semaphore_signal(barrier, inc=1, device_id={'sp': peer}, device_id_type=MESH)
    pl.semaphore_wait(barrier, 6)

    def own_lanes(x):
        return jnp.where(core == 0, x, pltpu.roll(x, 112, 1))

    c1 = (remote(o_ref.at[dyn((1 - core) * HALF_ROWS, HALF_ROWS)], c1_o, c_ssem.at[0], c_rsem.at[0], {'sp': partner}),
          remote(st_ref, c1_s, c_ssem.at[1], c_rsem.at[1], {'sp': partner}))
    for copy in c1:
        copy.start()
    for copy in smalls:
        copy.wait()
    for n, buf in enumerate((bo_buf, g_buf, b_buf, b1_buf, b2_buf)):
        rows_ref[n] = as_row(buf)
    m_a, l_a = own_lanes(st_ref[0]), own_lanes(st_ref[1])
    for copy in c1:
        copy.wait_recv()
    m_b, l_b = own_lanes(c1_s[0]), own_lanes(c1_s[1])
    m_ab = jnp.maximum(m_a, m_b)
    f_a, f_b = jnp.exp(m_a - m_ab), jnp.exp(m_b - m_ab)
    l_ab = f_a * l_a + f_b * l_b
    cs_s[0] = m_ab
    cs_s[1] = l_ab
    for t in range(HALF_ROWS):
        cs_o[t] = o_ref[core * HALF_ROWS + t] * f_a[:, t:t + 1] + c1_o[t] * f_b[:, t:t + 1]

    c2 = (remote(cs_s, c2_s, c_ssem.at[2], c_rsem.at[2], {'sp': across}),
          remote(cs_o, c2_o, c_ssem.at[3], c_rsem.at[3], {'sp': across}))
    for copy in c2:
        copy.start()
    c2[0].wait_recv()
    m_c, l_c = c2_s[0], c2_s[1]
    m_all = jnp.maximum(m_ab, m_c)
    f_ab, f_c = jnp.exp(m_ab - m_all), jnp.exp(m_c - m_all)
    denom = f_ab * l_ab + f_c * l_c
    c2[1].wait_recv()
    for t in range(HALF_ROWS):
        mixed = cs_o[t] * f_ab[:, t:t + 1] + c2_o[t] * f_c[:, t:t + 1]
        a_f32[t] = mixed / denom[:, t:t + 1]
    for h in range(HEADS):
        a_bf[:, h * 128:(h + 1) * 128] = a_f32[:, h, :].astype(BF16)

    def scatter(ar, n, k):
        return remote(rs_send.at[ar, n], rs_recv.at[ar, n], rs_ssem.at[ar, n], rs_rsem.at[ar, n], {'tp': zpeer[k]})

    def gathered(ar, s, zz, n, device):
        return remote(gat.at[ar, s, zz], gat.at[ar, s, zz], g_ssem.at[ar, n], g_rsem.at[ar, s, zz], device)

    def share(ar, block):
        gat[ar, sp, z] = block
        sends = [gathered(ar, sp, z, n, {'tp': zpeer[k]}) for n, k in enumerate(SEND_ORDER)]
        for copy in sends:
            copy.start()

        def pass_on(zz, n):
            out = [gathered(ar, sp, zz, n + i, {'sp': peer}) for i, peer in enumerate((across, across_other, partner))]
            for copy in out:
                copy.start()
            return out

        sends += pass_on(z, 3)
        for i, k in enumerate((1, 2, 3)):
            gathered(ar, sp, zpeer[k], 0, {'tp': zpeer[k]}).wait_recv()
            sends += pass_on(zpeer[k], 6 + 3 * i)
        for k in (0, 1, 2, 3):
            for peer in (partner, across, across_other):
                gathered(ar, peer, zpeer[k], 0, {'sp': peer}).wait_recv()
        return sends

    row0 = core * HALF_ROWS
    col0 = yy * 2048 + z * 512
    my_rows = dyn(row0, HALF_ROWS)
    my_cols = dyn(col0, 512)

    for j in range(4):
        loads[j].wait()
    pending = []
    for n, k in enumerate(SEND_ORDER):
        rs_send[0, n] = jnp.dot(a_bf[...], wo_buf[zpeer[k]], preferred_element_type=F32)
        copy = scatter(0, n, k)
        copy.start()
        pending.append(copy)
    total = jnp.dot(a_bf[...], wo_buf[z], preferred_element_type=F32)
    for copy in pending:
        copy.wait_recv()
    total = total + rs_recv[0, 0] + rs_recv[0, 1] + rs_recv[0, 2]
    resid = (hid_ref[my_rows, my_cols].astype(F32) + total + rows_ref[0, :, my_cols]).astype(BF16).astype(F32)
    pending += share(0, resid)

    for c in range(2):
        slots = [(2 * y + c, zz) for y in range(2) for zz in range(4)]
        acc = None
        for s, zz in slots:
            acc = gat[0, s, zz] if acc is None else acc + gat[0, s, zz]
        mean = jnp.sum(acc, -1, keepdims=True) * (1.0 / DIM)
        acc = None
        for s, zz in slots:
            centered = gat[0, s, zz] - mean
            acc = centered * centered if acc is None else acc + centered * centered
        scale = lax.rsqrt(jnp.sum(acc, -1, keepdims=True) * (1.0 / DIM) + LN_EPS)
        for s, zz in slots:
            cols = pl.ds((s // 2) * 2048 + zz * 512, 512)
            y_bf[c * 16:(c + 1) * 16, cols] = ((gat[0, s, zz] - mean) * scale * rows_ref[1, :, cols]
                                               + rows_ref[2, :, cols]).astype(BF16)

    for j in range(4):
        loads[4 + j].wait()
        part = jnp.dot(y_bf[...], w1_buf[j], preferred_element_type=F32)
        part = part + rows_ref[3, :, dyn(core * 2048 + j * 512, 512)]
        u_bf[:, j * 512:(j + 1) * 512] = jnp.maximum(part, 0.0).astype(BF16)
    for j in range(4):
        loads[8 + j].wait()
    swaps = []
    scatters = []

    def merge(n):
        swaps[n].wait_recv()
        merged = m_own[n] + m_recv[n]
        if n < 3:
            rs_send[1, n] = merged
            copy = scatter(1, n, SEND_ORDER[n])
            copy.start()
            scatters.append(copy)
        return merged

    for n, k in enumerate(SEND_ORDER + (0,)):
        part = jnp.dot(u_bf[...], w2_buf[zpeer[k]], preferred_element_type=F32)
        m_send[n] = jnp.where(core == 0, part[16:], part[:16])
        m_own[n] = jnp.where(core == 0, part[:16], part[16:])
        copy = remote(m_send.at[n], m_recv.at[n], m_ssem.at[n], m_rsem.at[n], {'sp': partner})
        copy.start()
        swaps.append(copy)
        if n >= 2:
            merge(n - 2)
    merge(2)
    total = merge(3)
    for copy in scatters:
        copy.wait_recv()
    total = total + rs_recv[1, 0] + rs_recv[1, 1] + rs_recv[1, 2]
    final = (resid + total + rows_ref[4, :, my_cols]).astype(BF16).astype(F32)
    pending += share(1, final)
    for s in range(4):
        for zz in range(4):
            out_ref[(s % 2) * 16:(s % 2) * 16 + 16, (s // 2) * 2048 + zz * 512:(s // 2) * 2048 + zz * 512 + 512] = (
                gat[1, s, zz].astype(BF16))

    for copy in (*c1, *c2, *pending, *swaps, *scatters):
        copy.wait_send()


def finish_call(o_part, stats, hidden, b_out, gain, bias, b_fc1, b_fc2, w_out, w_fc1, w_fc2):
    dma = pltpu.SemaphoreType.DMA
    return pl.pallas_call(
        finish_kernel,
        out_shape=jax.ShapeDtypeStruct((ROWS, DIM), BF16),
        in_specs=[vmem_spec()] * 2 + [any_spec()] * 9,
        out_specs=vmem_spec(),
        scratch_shapes=[
            pltpu.VMEM((ROWS, DIM), BF16),
            *[pltpu.VMEM((DIM,), BF16) for _ in range(5)],
            pltpu.VMEM((5, 1, DIM), F32),
            dma((6,)),
            pltpu.VMEM((4, 1024, 512), BF16),
            pltpu.VMEM((4, DIM, 512), BF16),
            pltpu.VMEM((4, 2048, 512), BF16),
            pltpu.VMEM((16, 8, 128), F32), pltpu.VMEM((2, 8, 128), F32),
            pltpu.VMEM((16, 8, 128), F32), pltpu.VMEM((2, 8, 128), F32),
            pltpu.VMEM((16, 8, 128), F32), pltpu.VMEM((2, 8, 128), F32),
            pltpu.VMEM((16, 8, 128), F32),
            pltpu.VMEM((16, 1024), BF16),
            pltpu.VMEM((2, 3, 16, 512), F32), pltpu.VMEM((2, 3, 16, 512), F32),
            pltpu.VMEM((4, 16, 512), F32), pltpu.VMEM((4, 16, 512), F32), pltpu.VMEM((4, 16, 512), F32),
            pltpu.VMEM((2, 4, 4, 16, 512), F32),
            pltpu.VMEM((ROWS, DIM), BF16),
            pltpu.VMEM((ROWS, 2048), BF16),
            dma((4,)), dma((4,)), dma((4,)), dma((4,)), dma((4,)), dma((2, 3)), dma((2, 3)),
            dma((4,)), dma((4,)), dma((2, 15)), dma((2, 4, 4)),
        ],
        compiler_params=pltpu.CompilerParams(collective_id=1, has_side_effects=True, vmem_limit_bytes=44 * MIB),
        name='finish',
    )(o_part, stats, hidden, b_out, gain, bias, b_fc1, b_fc2, w_out, w_fc1, w_fc2)


def solution(mesh):
    cache_spec = P('dp', 'tp', 'sp', None)
    col_spec = P(None, 'tp')
    row_spec = P('tp', None)
    in_specs = (P('dp', None), P('dp'), cache_spec, cache_spec, P(), P(), col_spec, P('tp'), col_spec, P('tp'),
                col_spec, P('tp'), row_spec, P(), P(), P(), col_spec, P('tp'), row_spec, P())
    out_specs = (P('dp', None), cache_spec, cache_spec)

    def local_layer(hidden, positions, k_cache, v_cache, ln1_gain, ln1_bias, w_query, b_query, w_key, b_key, w_value, b_value, w_out, b_out, ln2_gain, ln2_bias, w_fc1, b_fc1, w_fc2, b_fc2):
        keep = lambda array: pltpu.with_memory_space_constraint(array, pltpu.HBM)
        qkv = qkv_call(*map(keep, (hidden, ln1_gain, ln1_bias, w_query, b_query, w_key, b_key, w_value, b_value)))
        k_next, v_next, o_part, stats = attn_call(positions, qkv, keep(k_cache), keep(v_cache))
        result = finish_call(o_part, stats, *map(keep, (hidden, b_out, ln2_gain, ln2_bias, b_fc1, b_fc2, w_out, w_fc1, w_fc2)))
        return result, k_next, v_next

    return jax.shard_map(local_layer, mesh=mesh, in_specs=in_specs, out_specs=out_specs, check_vma=False)
```

time: 181 us -> 71 us (0.39)
  waiting for transfers between devices: 77.7 us -> 0 us
  Pallas kernels: 0 us -> 69.9 us
  matrix products: 52.7 us -> 0 us
  other arithmetic: 18.9 us -> 0 us
  between operations: 14.4 us -> 0.67 us
  blocking collectives: 11.6 us -> 0 us
  local copies, waits for them, and re-layouts: 4.81 us -> 0.71 us
    psum x2 -> x0, waiting for transfers between devices: 77.7 us -> none  [the longest x1 39.3 us: finish_layer(): attn_sum = lax.psum(attn_part, 'tp')]
    pallas_call x0 -> x3, Pallas kernels: none -> 69.9 us  [the longest x1 47.9 us: finish_call(): pl.pallas_call(finish_kernel, out_shape=jax.ShapeDtypeStruct((ROWS, DIM),...]
    dot_general x7 -> x0, matrix products: 52.7 us -> none  [the longest x1 25.1 us: finish_layer(): mlp_part = jnp.dot(activated, w_fc2, preferred_element_type=jnp.float32)]
    all_gather x1 -> x0, blocking collectives: 11.6 us -> none  [local_layer(): gathered = lax.all_gather(block_stats, 'sp')]
    select_n x1 -> x0, other arithmetic: 9.27 us -> none  [local_layer(): v_next = jnp.where(at_slot, new_value[:, :, None, :], v_cache)]
    reduce_sum x6 -> x0, other arithmetic: 4.76 us -> none  [the longest x2 2.47 us: layer_norm(): centered = as_f32 - as_f32.mean(-1, keepdims=True)]
    convert_element_type x13 -> x0, other arithmetic: 4.22 us -> none  [the longest x1 1.81 us: finish_layer(): (resid_one.astype(jnp.float32) + mlp_sum + b_fc2.astype(jnp.float32)).ast...]
    unnamed x26 -> x3, local copies, waits for them, and re-layouts: 3.81 us -> 0.71 us
  transfers between devices with their start and end apart: 2 -> 0, of which waited for: 2 -> 0; matrix products, arithmetic and copies ran while one was open for 0% -> 0% of each run, Pallas kernels for 0% -> 0%
where the time goes in v1:
time: 71 us; the launch traced here: 71.2 us
  Pallas kernels  69.9 us (98%)
  local copies, waits for them, and re-layouts  0.71 us (1%)
    pallas_call x1, Pallas kernels, finish_call(): pl.pallas_call(finish_kernel, out_shape=jax.ShapeDtypeStruct((ROWS, DIM),...  47.9 us
    pallas_call x1, Pallas kernels, attn_call(): pl.pallas_call(attn_kernel, out_shape=(cache, cache, jax.ShapeDtypeStruct...  12.7 us
    pallas_call x1, Pallas kernels, qkv_call(): pl.pallas_call(qkv_kernel, out_shape=jax.ShapeDtypeStruct((3, HEADS, ROWS...  9.19 us

profile of v1, /device:TPU:0, one launch (start us, length us, event | category | flops | bytes accessed | tf_op | source)
XLA Modules:
  0.0 71.2 jit_solution(5800152559535362765)
XLA Ops:
  0.6 0.0 copy-start
  0.6 9.2 %qkv.1.qkv_ref = f32[3,8,32,128]{3,2,1,0:T(8,128)S(1)} custom-call(bf16[32,4096]{1,0:T(8,128)(2,1)} %hid_hbm.1, bf16[4096]{0:T(1024)(128)(2,1)} %g_hbm.2, bf16[4096]{0:T(1024)(128)(2,1)} %b_hbm.2, bf16[4096,1024]{1,0:T(8,128)(2,1)} %wq_ref.1, bf16[4096,1024]{1,0:T(8,128)(2,1)} %wk_ref.1, bf16[4096,1024]{1,0:T(8,128)(2,1)} %wv_ref.1, bf16[1024]{0:T(1024)(128)(2,1)} %bq_hbm.1, ...), custom_call_target="tpu_custom_call" | custom-call | tf_op jit(solution)/shard_map/qkv/pallas_call | solution.py:105
  9.8 0.0 copy-done
  9.9 12.7 %attn.1 = (bf16[32,8,128,128]{3,2,1,0:T(8,128)(2,1)}, bf16[32,8,128,128]{3,2,1,0:T(8,128)(2,1)}, f32[32,8,128]{2,1,0:T(8,128)S(1)}, f32[2,8,128]{2,1,0:T(8,128)S(1)}) custom-call(s32[32]{0:T(128)S(1)} %copy-done, f32[3,8,32,128]{3,2,1,0:T(8,128)S(1)} %qkv.1.qkv_ref, bf16[32,8,128,128]{3,2,1,0:T(8,128)(2,1)} %k_hbm.1, bf16[32,8,128,128]{3,2,1,0:T(8,128)(2,1)} %v_hbm.1), custom_call_target="tpu_custom_call" | custom-call | tf_op jit(solution)/shard_map/attn/pallas_call | solution.py:223
  22.6 47.9 %finish.1 = bf16[32,4096]{1,0:T(8,128)(2,1)S(1)} custom-call(f32[32,8,128]{2,1,0:T(8,128)S(1)} %get-tuple-element.7.o_ref, f32[2,8,128]{2,1,0:T(8,128)S(1)} %get-tuple-element.8.st_ref, bf16[32,4096]{1,0:T(8,128)(2,1)} %hid_hbm.1, bf16[4096]{0:T(1024)(128)(2,1)} %bo_hbm.1, bf16[4096]{0:T(1024)(128)(2,1)} %g_hbm.3, bf16[4096]{0:T(1024)(128)(2,1)} %b_hbm.3, ...), custom_call_target="tpu_custom_call" | custom-call | tf_op jit(solution)/shard_map/finish/pallas_call | solution.py:431
  70.5 0.7 copy.24
Async XLA Ops:
  0.6 9.2 %copy-start = (s32[32]{0:T(128)S(1)}, s32[32]{0:T(128)}, u32[]{:S(2)}) copy-start(s32[32]{0:T(128)} %pos_ref.1) | copy-start | bytes 388

commit v2 on v1

--- a/solution.py
+++ b/solution.py
@@ -18,34 +18,27 @@
 BLOCK_LEN = 128
 MIB = 1 << 20
 
-
 def any_spec():
     return pl.BlockSpec(memory_space=pltpu.HBM)
 
-
 def vmem_spec():
     return pl.BlockSpec(memory_space=pltpu.VMEM)
-
 
 def remote(src, dst, send_sem, recv_sem, device):
     return pltpu.make_async_remote_copy(src_ref=src, dst_ref=dst, send_sem=send_sem, recv_sem=recv_sem,
                                         device_id=device, device_id_type=MESH)
 
-
 def dyn(start, size):
     return pl.ds(pl.multiple_of(start, size), size)
 
-
 QKV_CHUNKS = 4
 QKV_ROWS = DIM // QKV_CHUNKS
 
-
 def as_row(vec_ref):
     return vec_ref[...].astype(F32)[None, :]
 
-
-def qkv_kernel(h_hbm, g_hbm, b_hbm, wq_ref, wk_ref, wv_ref, bq_hbm, bk_hbm, bv_hbm, out_ref,
-               h_buf, g_buf, b_buf, bq_buf, bk_buf, bv_buf, bias_rows, wbuf, norm, send, recv, vsem, wsem, ssem, rsem):
+def qkv_kernel(h_hbm, g_hbm, b_hbm, wq_ref, wk_ref, wv_ref, bq_hbm, bk_hbm, bv_hbm, k_hbm, out_ref, k_vmem,
+               h_buf, g_buf, b_buf, bq_buf, bk_buf, bv_buf, bias_rows, wbuf, norm, send, recv, vsem, wsem, ksem, ssem, rsem):
     smalls = [pltpu.make_async_copy(src, dst, vsem.at[n]) for n, (src, dst) in enumerate((
         (h_hbm, h_buf), (g_hbm, g_buf), (b_hbm, b_buf), (bq_hbm, bq_buf), (bk_hbm, bk_buf), (bv_hbm, bv_buf)))]
     for copy in smalls:
@@ -59,13 +52,20 @@
         for j in range(QKV_CHUNKS):
             rows = pl.ds(j * QKV_ROWS, QKV_ROWS)
             copy = pltpu.make_async_copy(weight.at[rows, cols], wbuf.at[i, rows, :], wsem.at[i, j])
-            copy.start()
+            copy.start(priority=1)
             copies.append(copy)
+    prefetch = []
+    for j in range(4):
+        rows = pl.ds(j * 8, 8)
+        copy = pltpu.make_async_copy(k_hbm.at[rows], k_vmem.at[rows], ksem.at[j])
+        copy.start(priority=1)
+        prefetch.append(copy)
     barrier = pltpu.get_barrier_semaphore()
     pl.semaphore_signal(barrier, inc=1, device_id={'sp': partner}, device_id_type=MESH)
 
     for copy in smalls:
         copy.wait()
+
     values = h_buf[...].astype(F32)
     centered = values - jnp.mean(values, -1, keepdims=True)
     variance = jnp.mean(centered * centered, -1, keepdims=True)
@@ -74,6 +74,7 @@
         bias_rows[i] = as_row(buf)
 
     pl.semaphore_wait(barrier, 1)
+
     sends = []
     for i in range(3):
         total = None
@@ -93,20 +94,23 @@
         sends.append(copy)
         for h in range(4):
             out_ref[i, core * 4 + h] = total[:, h * 128:(h + 1) * 128]
+
     for i in range(3):
         sends[i].wait_recv()
         for h in range(4):
             out_ref[i, (1 - core) * 4 + h] = recv[i, h]
+
     for i in range(3):
         sends[i].wait_send()
-
-
-def qkv_call(hidden, gain, bias, w_query, b_query, w_key, b_key, w_value, b_value):
+    for copy in prefetch:
+        copy.wait()
+
+def qkv_call(hidden, gain, bias, w_query, b_query, w_key, b_key, w_value, b_value, k_cache):
     return pl.pallas_call(
         qkv_kernel,
-        out_shape=jax.ShapeDtypeStruct((3, HEADS, ROWS, HEAD_DIM), F32),
-        in_specs=[any_spec()] * 9,
-        out_specs=vmem_spec(),
+        out_shape=(jax.ShapeDtypeStruct((3, HEADS, ROWS, HEAD_DIM), F32), pltpu.VMEM(k_cache.shape, BF16)),
+        in_specs=[any_spec()] * 10,
+        out_specs=(vmem_spec(), vmem_spec()),
         scratch_shapes=[
             pltpu.VMEM((ROWS, DIM), BF16),
             pltpu.VMEM((DIM,), BF16), pltpu.VMEM((DIM,), BF16),
@@ -118,19 +122,18 @@
             pltpu.VMEM((3, 4, ROWS, 128), F32),
             pltpu.SemaphoreType.DMA((6,)),
             pltpu.SemaphoreType.DMA((3, QKV_CHUNKS)),
+            pltpu.SemaphoreType.DMA((4,)),
             pltpu.SemaphoreType.DMA((3,)),
             pltpu.SemaphoreType.DMA((3,)),
         ],
-        compiler_params=pltpu.CompilerParams(collective_id=0, has_side_effects=True, vmem_limit_bytes=24 * MIB),
+        compiler_params=pltpu.CompilerParams(collective_id=0, has_side_effects=True, vmem_limit_bytes=16 * MIB),
         name='qkv',
-    )(hidden, gain, bias, w_query, w_key, w_value, b_query, b_key, b_value)
-
+    )(hidden, gain, bias, w_query, w_key, w_value, b_query, b_key, b_value, k_cache)
 
 CHUNK = 4
 NUM_CHUNKS = ROWS // CHUNK
 
-
-def attn_kernel(pos_ref, qkv_ref, k_hbm, v_hbm, k_out, v_out, o_ref, st_ref, kbuf, vbuf, qs, kin, vin, kdone, vdone):
+def attn_kernel(pos_ref, qkv_ref, k_in, v_hbm, k_out, v_out, o_ref, st_ref, kbuf, vbuf, qs, vin, kdone, vdone):
     base = lax.axis_index('sp') * BLOCK_LEN
 
     def chunk_copy(src, dst, sem, p):
@@ -138,8 +141,8 @@
         return pltpu.make_async_copy(src.at[rows], dst.at[rows], sem.at[p])
 
     for p in range(NUM_CHUNKS):
-        chunk_copy(k_hbm, kbuf, kin, p).start()
         chunk_copy(v_hbm, vbuf, vin, p).start()
+
     for i in range(3):
         qs[i] = jnp.swapaxes(qkv_ref[i], 0, 1)
 
@@ -161,7 +164,6 @@
 
     def body(p, carry):
         mm, ll = carry
-        chunk_copy(k_hbm, kbuf, kin, p).wait()
         chunk_copy(v_hbm, vbuf, vin, p).wait()
         locals_ = [pos_ref[p * CHUNK + t] - base for t in range(CHUNK)]
         for t in range(CHUNK):
@@ -213,35 +215,32 @@
     mm, ll = lax.fori_loop(0, NUM_CHUNKS, body, (zeros, zeros))
     st_ref[0] = mm
     st_ref[1] = ll
+
     for p in range(NUM_CHUNKS):
         chunk_copy(kbuf, k_out, kdone, p).wait()
         chunk_copy(vbuf, v_out, vdone, p).wait()
-
 
 def attn_call(positions, qkv, k_cache, v_cache):
     cache = jax.ShapeDtypeStruct(k_cache.shape, BF16)
     return pl.pallas_call(
         attn_kernel,
         out_shape=(cache, cache, jax.ShapeDtypeStruct((ROWS, HEADS, HEAD_DIM), F32),
-                   jax.ShapeDtypeStruct((2, HEADS, 128), F32)),
-        in_specs=[pl.BlockSpec(memory_space=pltpu.SMEM), vmem_spec(), any_spec(), any_spec()],
-        out_specs=(any_spec(), any_spec(), vmem_spec(), vmem_spec()),
+                   jax.ShapeDtypeStruct((2, HEADS, 128), F32), pltpu.VMEM(k_cache.shape, BF16)),
+        in_specs=[pl.BlockSpec(memory_space=pltpu.SMEM), vmem_spec(), vmem_spec(), any_spec()],
+        out_specs=(any_spec(), any_spec(), vmem_spec(), vmem_spec(), vmem_spec()),
+        input_output_aliases={2: 4},
         scratch_shapes=[
-            pltpu.VMEM(k_cache.shape, BF16),
             pltpu.VMEM(k_cache.shape, BF16),
             pltpu.VMEM((3, ROWS, HEADS, HEAD_DIM), F32),
             pltpu.SemaphoreType.DMA((NUM_CHUNKS,)),
             pltpu.SemaphoreType.DMA((NUM_CHUNKS,)),
             pltpu.SemaphoreType.DMA((NUM_CHUNKS,)),
-            pltpu.SemaphoreType.DMA((NUM_CHUNKS,)),
         ],
-        compiler_params=pltpu.CompilerParams(vmem_limit_bytes=24 * MIB),
+        compiler_params=pltpu.CompilerParams(vmem_limit_bytes=16 * MIB),
         name='attn',
     )(positions, qkv, k_cache, v_cache)
 
-
 SEND_ORDER = (3, 2, 1)
-
 
 def finish_kernel(o_ref, st_ref, hid_hbm, bo_hbm, g_hbm, b_hbm, b1_hbm, b2_hbm, wo_hbm, w1_hbm, w2_hbm, out_ref,
                   hid_ref, bo_buf, g_buf, b_buf, b1_buf, b2_buf, rows_ref, small_sem,
@@ -261,6 +260,8 @@
         (hid_hbm, hid_ref), (bo_hbm, bo_buf), (g_hbm, g_buf), (b_hbm, b_buf), (b1_hbm, b1_buf), (b2_hbm, b2_buf)))]
     for copy in smalls:
         copy.start()
+    inner = (z == 0) | (z == 3)
+    nearest = (zpeer[1], jnp.where(inner, zpeer[3], zpeer[2]), jnp.where(inner, zpeer[2], zpeer[3]))
     loads = []
     for j in range(4):
         loads.append(pltpu.make_async_copy(wo_hbm.at[:, dyn(yy * 2048 + j * 512, 512)], wo_buf.at[j], wo_sem.at[j]))
@@ -269,14 +270,12 @@
     for j in range(4):
         loads.append(pltpu.make_async_copy(w2_hbm.at[dyn(core * 2048, 2048), dyn(yy * 2048 + j * 512, 512)],
                                            w2_buf.at[j], w2_sem.at[j]))
-    for load in loads:
-        load.start()
-
     barrier = pltpu.get_barrier_semaphore()
     for k in (1, 2, 3):
         pl.semaphore_signal(barrier, inc=1, device_id={'tp': zpeer[k]}, device_id_type=MESH)
     for peer in (partner, across, across_other):
         pl.semaphore_signal(barrier, inc=1, device_id={'sp': peer}, device_id_type=MESH)
+
     pl.semaphore_wait(barrier, 6)
 
     def own_lanes(x):
@@ -286,6 +285,8 @@
           remote(st_ref, c1_s, c_ssem.at[1], c_rsem.at[1], {'sp': partner}))
     for copy in c1:
         copy.start()
+    for load in loads[:4]:
+        load.start(priority=1)
     for copy in smalls:
         copy.wait()
     for n, buf in enumerate((bo_buf, g_buf, b_buf, b1_buf, b2_buf)):
@@ -306,8 +307,11 @@
           remote(cs_o, c2_o, c_ssem.at[3], c_rsem.at[3], {'sp': across}))
     for copy in c2:
         copy.start()
+    for load in loads[4:6]:
+        load.start(priority=1)
     c2[0].wait_recv()
     m_c, l_c = c2_s[0], c2_s[1]
+
     m_all = jnp.maximum(m_ab, m_c)
     f_ab, f_c = jnp.exp(m_ab - m_all), jnp.exp(m_c - m_all)
     denom = f_ab * l_ab + f_c * l_c
@@ -337,9 +341,9 @@
             return out
 
         sends += pass_on(z, 3)
-        for i, k in enumerate((1, 2, 3)):
-            gathered(ar, sp, zpeer[k], 0, {'tp': zpeer[k]}).wait_recv()
-            sends += pass_on(zpeer[k], 6 + 3 * i)
+        for i, peer in enumerate(nearest):
+            gathered(ar, sp, peer, 0, {'tp': peer}).wait_recv()
+            sends += pass_on(peer, 6 + 3 * i)
         for k in (0, 1, 2, 3):
             for peer in (partner, across, across_other):
                 gathered(ar, peer, zpeer[k], 0, {'sp': peer}).wait_recv()
@@ -358,13 +362,19 @@
         copy = scatter(0, n, k)
         copy.start()
         pending.append(copy)
+    for load in loads[6:8]:
+        load.start(priority=1)
     total = jnp.dot(a_bf[...], wo_buf[z], preferred_element_type=F32)
+
     for copy in pending:
         copy.wait_recv()
     total = total + rs_recv[0, 0] + rs_recv[0, 1] + rs_recv[0, 2]
     resid = (hid_ref[my_rows, my_cols].astype(F32) + total + rows_ref[0, :, my_cols]).astype(BF16).astype(F32)
+
     pending += share(0, resid)
 
+    for load in loads[8:]:
+        load.start(priority=1)
     for c in range(2):
         slots = [(2 * y + c, zz) for y in range(2) for zz in range(4)]
         acc = None
@@ -386,6 +396,7 @@
         part = jnp.dot(y_bf[...], w1_buf[j], preferred_element_type=F32)
         part = part + rows_ref[3, :, dyn(core * 2048 + j * 512, 512)]
         u_bf[:, j * 512:(j + 1) * 512] = jnp.maximum(part, 0.0).astype(BF16)
+
     for j in range(4):
         loads[8 + j].wait()
     swaps = []
@@ -412,11 +423,14 @@
             merge(n - 2)
     merge(2)
     total = merge(3)
+
     for copy in scatters:
         copy.wait_recv()
     total = total + rs_recv[1, 0] + rs_recv[1, 1] + rs_recv[1, 2]
     final = (resid + total + rows_ref[4, :, my_cols]).astype(BF16).astype(F32)
+
     pending += share(1, final)
+
     for s in range(4):
         for zz in range(4):
             out_ref[(s % 2) * 16:(s % 2) * 16 + 16, (s // 2) * 2048 + zz * 512:(s // 2) * 2048 + zz * 512 + 512] = (
@@ -424,7 +438,6 @@
 
     for copy in (*c1, *c2, *pending, *swaps, *scatters):
         copy.wait_send()
-
 
 def finish_call(o_part, stats, hidden, b_out, gain, bias, b_fc1, b_fc2, w_out, w_fc1, w_fc2):
     dma = pltpu.SemaphoreType.DMA
@@ -458,7 +471,6 @@
         name='finish',
     )(o_part, stats, hidden, b_out, gain, bias, b_fc1, b_fc2, w_out, w_fc1, w_fc2)
 
-
 def solution(mesh):
     cache_spec = P('dp', 'tp', 'sp', None)
     col_spec = P(None, 'tp')
@@ -469,8 +481,8 @@
 
     def local_layer(hidden, positions, k_cache, v_cache, ln1_gain, ln1_bias, w_query, b_query, w_key, b_key, w_value, b_value, w_out, b_out, ln2_gain, ln2_bias, w_fc1, b_fc1, w_fc2, b_fc2):
         keep = lambda array: pltpu.with_memory_space_constraint(array, pltpu.HBM)
-        qkv = qkv_call(*map(keep, (hidden, ln1_gain, ln1_bias, w_query, b_query, w_key, b_key, w_value, b_value)))
-        k_next, v_next, o_part, stats = attn_call(positions, qkv, keep(k_cache), keep(v_cache))
+        qkv, k_vmem = qkv_call(*map(keep, (hidden, ln1_gain, ln1_bias, w_query, b_query, w_key, b_key, w_value, b_value, k_cache)))
+        k_next, v_next, o_part, stats, _ = attn_call(positions, qkv, k_vmem, keep(v_cache))
         result = finish_call(o_part, stats, *map(keep, (hidden, b_out, ln2_gain, ln2_bias, b_fc1, b_fc2, w_out, w_fc1, w_fc2)))
         return result, k_next, v_next
 

time: 71 us -> 61.6 us (0.87)
  Pallas kernels: 69.9 us -> 60.2 us
    pallas_call x1, Pallas kernels: 47.9 us -> 42.9 us  [finish_call(): pl.pallas_call(finish_kernel, out_shape=jax.ShapeDtypeStruct((ROWS, DIM),...]
    pallas_call x1, Pallas kernels: 12.7 us -> 8.6 us  [attn_call(): pl.pallas_call(attn_kernel, out_shape=(cache, cache, jax.ShapeDtypeStruct...]
where the time goes in v2:
time: 61.6 us
  Pallas kernels  60.2 us (98%)
  local copies, waits for them, and re-layouts  0.71 us (1%)
  between operations  0.67 us (1%)
    pallas_call x1, Pallas kernels, finish_call(): pl.pallas_call(finish_kernel, out_shape=jax.ShapeDtypeStruct((ROWS, DIM),...  42.9 us
    pallas_call x1, Pallas kernels, qkv_call(): pl.pallas_call(qkv_kernel, out_shape=(jax.ShapeDtypeStruct((3, HEADS, ROW...  8.75 us
    pallas_call x1, Pallas kernels, attn_call(): pl.pallas_call(attn_kernel, out_shape=(cache, cache, jax.ShapeDtypeStruct...  8.6 us

profile of v2, /device:TPU:0, one launch (start us, length us, event | category | flops | bytes accessed | tf_op | source)
XLA Modules:
  0.0 61.6 jit_solution(2804135318087939623)
XLA Ops:
  0.6 0.0 copy-start
  0.6 8.7 %qkv.1 = (f32[3,8,32,128]{3,2,1,0:T(8,128)S(1)}, bf16[32,8,128,128]{3,2,1,0:T(8,128)(2,1)S(1)}) custom-call(bf16[32,4096]{1,0:T(8,128)(2,1)} %hid_hbm.1, bf16[4096]{0:T(1024)(128)(2,1)} %g_hbm.2, bf16[4096]{0:T(1024)(128)(2,1)} %b_hbm.2, bf16[4096,1024]{1,0:T(8,128)(2,1)} %wq_ref.1, bf16[4096,1024]{1,0:T(8,128)(2,1)} %wk_ref.1, bf16[4096,1024]{1,0:T(8,128)(2,1)} %wv_ref.1, ...), custom_call_target="tpu_custom_call" | custom-call | tf_op jit(solution)/shard_map/qkv/pallas_call | solution.py:109
  9.4 0.0 copy-done
  9.4 8.6 %attn.1 = (bf16[32,8,128,128]{3,2,1,0:T(8,128)(2,1)}, bf16[32,8,128,128]{3,2,1,0:T(8,128)(2,1)}, f32[32,8,128]{2,1,0:T(8,128)S(1)}, f32[2,8,128]{2,1,0:T(8,128)S(1)}, bf16[32,8,128,128]{3,2,1,0:T(8,128)(2,1)S(1)}) custom-call(s32[32]{0:T(128)S(1)} %copy-done, f32[3,8,32,128]{3,2,1,0:T(8,128)S(1)} %get-tuple-element.9.qkv_ref, ...), custom_call_target="tpu_custom_call", output_to_operand_aliasing={{4}: (2, {})} | custom-call | tf_op jit(solution)/shard_map/attn/pallas_call | solution.py:225
  18.0 42.9 %finish.1 = bf16[32,4096]{1,0:T(8,128)(2,1)S(1)} custom-call(f32[32,8,128]{2,1,0:T(8,128)S(1)} %get-tuple-element.11.o_ref, f32[2,8,128]{2,1,0:T(8,128)S(1)} %get-tuple-element.12.st_ref, bf16[32,4096]{1,0:T(8,128)(2,1)} %hid_hbm.1, bf16[4096]{0:T(1024)(128)(2,1)} %bo_hbm.1, bf16[4096]{0:T(1024)(128)(2,1)} %g_hbm.3, bf16[4096]{0:T(1024)(128)(2,1)} %b_hbm.3, ...), custom_call_target="tpu_custom_call" | custom-call | tf_op jit(solution)/shard_map/finish/pallas_call | solution.py:444
  60.9 0.7 %copy.26 = bf16[32,4096]{1,0:T(8,128)(2,1)} copy(bf16[32,4096]{1,0:T(8,128)(2,1)S(1)} %finish.1) | data formatting | bytes 524288
Async XLA Ops:
  0.6 8.8 %copy-start = (s32[32]{0:T(128)S(1)}, s32[32]{0:T(128)}, u32[]{:S(2)}) copy-start(s32[32]{0:T(128)} %pos_ref.1) | copy-start | bytes 388

commit v3 on v2

--- a/solution.py
+++ b/solution.py
@@ -33,6 +33,7 @@
 
 QKV_CHUNKS = 4
 QKV_ROWS = DIM // QKV_CHUNKS
+PREFETCH_AT = (1, 3)
 
 def as_row(vec_ref):
     return vec_ref[...].astype(F32)[None, :]
@@ -58,7 +59,6 @@
     for j in range(4):
         rows = pl.ds(j * 8, 8)
         copy = pltpu.make_async_copy(k_hbm.at[rows], k_vmem.at[rows], ksem.at[j])
-        copy.start(priority=1)
         prefetch.append(copy)
     barrier = pltpu.get_barrier_semaphore()
     pl.semaphore_signal(barrier, inc=1, device_id={'sp': partner}, device_id_type=MESH)
@@ -80,6 +80,9 @@
         total = None
         for j in range(QKV_CHUNKS):
             copies[i * QKV_CHUNKS + j].wait()
+            if (i, j) == PREFETCH_AT:
+                for copy in prefetch:
+                    copy.start(priority=1)
             rows = pl.ds(j * QKV_ROWS, QKV_ROWS)
             part = jnp.dot(norm[:, rows], wbuf[i, rows, :], preferred_element_type=F32)
             total = part if total is None else total + part
@@ -240,13 +243,15 @@
         name='attn',
     )(positions, qkv, k_cache, v_cache)
 
-SEND_ORDER = (3, 2, 1)
+SEND_INNER = (2, 3, 1)
+SEND_OUTER = (1, 2, 3)
 
 def finish_kernel(o_ref, st_ref, hid_hbm, bo_hbm, g_hbm, b_hbm, b1_hbm, b2_hbm, wo_hbm, w1_hbm, w2_hbm, out_ref,
                   hid_ref, bo_buf, g_buf, b_buf, b1_buf, b2_buf, rows_ref, small_sem,
                   wo_buf, w1_buf, w2_buf, c1_o, c1_s, cs_o, cs_s, c2_o, c2_s, a_f32, a_bf, rs_send, rs_recv,
-                  m_own, m_send, m_recv, gat, y_bf, u_bf,
-                  wo_sem, w1_sem, w2_sem, c_ssem, c_rsem, rs_ssem, rs_rsem, m_ssem, m_rsem, g_ssem, g_rsem):
+                  u_send, u_recv, gat, gat2, y_bf, u_bf, x_bf,
+                  wo_sem, w1_sem, w2_sem, c_ssem, c_rsem, rs_ssem, rs_rsem, m_ssem, m_rsem,
+                  g_ssem, g_rsem, g2_ssem, g2_rsem):
     z = lax.axis_index('tp')
     sp = lax.axis_index('sp')
     core = lax.rem(sp, 2)
@@ -254,22 +259,31 @@
     partner = sp + 1 - 2 * core
     across = lax.rem(sp + 2, 4)
     across_other = lax.rem(partner + 2, 4)
-    zpeer = {1: z + 1 - 2 * lax.rem(z, 2), 2: lax.rem(z + 2, 4), 3: 3 - z, 0: z}
+    zpeer = {1: z + 1 - 2 * lax.rem(z, 2), 2: lax.rem(z + 2, 4), 3: 3 - z}
+    inner = (z == 0) | (z == 3)
+    step = [jnp.where(inner, a, b) for a, b in zip(SEND_INNER, SEND_OUTER)]
+    target = [jnp.where(inner, zpeer[a], zpeer[b]) for a, b in zip(SEND_INNER, SEND_OUTER)]
+    nearest = (zpeer[1], jnp.where(inner, zpeer[3], zpeer[2]), jnp.where(inner, zpeer[2], zpeer[3]))
 
     smalls = [pltpu.make_async_copy(src, dst, small_sem.at[n]) for n, (src, dst) in enumerate((
         (hid_hbm, hid_ref), (bo_hbm, bo_buf), (g_hbm, g_buf), (b_hbm, b_buf), (b1_hbm, b1_buf), (b2_hbm, b2_buf)))]
     for copy in smalls:
         copy.start()
-    inner = (z == 0) | (z == 3)
-    nearest = (zpeer[1], jnp.where(inner, zpeer[3], zpeer[2]), jnp.where(inner, zpeer[2], zpeer[3]))
-    loads = []
+    wo_loads, w1_loads, w2_loads = [], [], []
     for j in range(4):
-        loads.append(pltpu.make_async_copy(wo_hbm.at[:, dyn(yy * 2048 + j * 512, 512)], wo_buf.at[j], wo_sem.at[j]))
-    for j in range(4):
-        loads.append(pltpu.make_async_copy(w1_hbm.at[:, dyn(core * 2048 + j * 512, 512)], w1_buf.at[j], w1_sem.at[j]))
-    for j in range(4):
-        loads.append(pltpu.make_async_copy(w2_hbm.at[dyn(core * 2048, 2048), dyn(yy * 2048 + j * 512, 512)],
-                                           w2_buf.at[j], w2_sem.at[j]))
+        cols = dyn(core * 2048 + j * 512, 512)
+        wo_loads.append(pltpu.make_async_copy(wo_hbm.at[:, cols], wo_buf.at[j], wo_sem.at[j]))
+        w1_loads.append(pltpu.make_async_copy(w1_hbm.at[:, cols], w1_buf.at[j], w1_sem.at[j]))
+    for half, rows in enumerate((core, 1 - core)):
+        for n, dest in enumerate((*target, z)):
+            w2_loads.append(pltpu.make_async_copy(
+                w2_hbm.at[dyn(rows * 2048, 2048), dyn(core * 2048 + dest * 512, 512)],
+                w2_buf.at[half, n], w2_sem.at[half, n]))
+
+    def begin(loads):
+        for load in loads:
+            load.start(priority=1)
+
     barrier = pltpu.get_barrier_semaphore()
     for k in (1, 2, 3):
         pl.semaphore_signal(barrier, inc=1, device_id={'tp': zpeer[k]}, device_id_type=MESH)
@@ -279,162 +293,163 @@
     pl.semaphore_wait(barrier, 6)
 
     def own_lanes(x):
-        return jnp.where(core == 0, x, pltpu.roll(x, 112, 1))
-
-    c1 = (remote(o_ref.at[dyn((1 - core) * HALF_ROWS, HALF_ROWS)], c1_o, c_ssem.at[0], c_rsem.at[0], {'sp': partner}),
-          remote(st_ref, c1_s, c_ssem.at[1], c_rsem.at[1], {'sp': partner}))
+        return jnp.where(yy == 0, x, pltpu.roll(x, 112, 1))
+
+    c1 = (remote(st_ref, c1_s, c_ssem.at[0], c_rsem.at[0], {'sp': across}),
+          remote(o_ref.at[dyn((1 - yy) * HALF_ROWS, HALF_ROWS)], c1_o, c_ssem.at[1], c_rsem.at[1], {'sp': across}))
     for copy in c1:
         copy.start()
-    for load in loads[:4]:
-        load.start(priority=1)
+    begin(wo_loads)
+    begin(w1_loads[:1])
     for copy in smalls:
         copy.wait()
     for n, buf in enumerate((bo_buf, g_buf, b_buf, b1_buf, b2_buf)):
         rows_ref[n] = as_row(buf)
     m_a, l_a = own_lanes(st_ref[0]), own_lanes(st_ref[1])
-    for copy in c1:
-        copy.wait_recv()
+    c1[0].wait_recv()
     m_b, l_b = own_lanes(c1_s[0]), own_lanes(c1_s[1])
     m_ab = jnp.maximum(m_a, m_b)
     f_a, f_b = jnp.exp(m_a - m_ab), jnp.exp(m_b - m_ab)
     l_ab = f_a * l_a + f_b * l_b
     cs_s[0] = m_ab
     cs_s[1] = l_ab
+    c1[1].wait_recv()
     for t in range(HALF_ROWS):
-        cs_o[t] = o_ref[core * HALF_ROWS + t] * f_a[:, t:t + 1] + c1_o[t] * f_b[:, t:t + 1]
-
-    c2 = (remote(cs_s, c2_s, c_ssem.at[2], c_rsem.at[2], {'sp': across}),
-          remote(cs_o, c2_o, c_ssem.at[3], c_rsem.at[3], {'sp': across}))
+        cs_o[t] = o_ref[yy * HALF_ROWS + t] * f_a[:, t:t + 1] + c1_o[t] * f_b[:, t:t + 1]
+
+    c2 = (remote(cs_s, c2_s, c_ssem.at[2], c_rsem.at[2], {'sp': partner}),
+          remote(cs_o, c2_o, c_ssem.at[3], c_rsem.at[3], {'sp': partner}))
     for copy in c2:
         copy.start()
-    for load in loads[4:6]:
-        load.start(priority=1)
+    begin(w1_loads[1:2])
     c2[0].wait_recv()
     m_c, l_c = c2_s[0], c2_s[1]
-
     m_all = jnp.maximum(m_ab, m_c)
     f_ab, f_c = jnp.exp(m_ab - m_all), jnp.exp(m_c - m_all)
-    denom = f_ab * l_ab + f_c * l_c
+    inv = 1.0 / (f_ab * l_ab + f_c * l_c)
+    f_ab, f_c = f_ab * inv, f_c * inv
     c2[1].wait_recv()
     for t in range(HALF_ROWS):
-        mixed = cs_o[t] * f_ab[:, t:t + 1] + c2_o[t] * f_c[:, t:t + 1]
-        a_f32[t] = mixed / denom[:, t:t + 1]
+        a_f32[t] = cs_o[t] * f_ab[:, t:t + 1] + c2_o[t] * f_c[:, t:t + 1]
     for h in range(HEADS):
         a_bf[:, h * 128:(h + 1) * 128] = a_f32[:, h, :].astype(BF16)
 
-    def scatter(ar, n, k):
-        return remote(rs_send.at[ar, n], rs_recv.at[ar, n], rs_ssem.at[ar, n], rs_rsem.at[ar, n], {'tp': zpeer[k]})
-
-    def gathered(ar, s, zz, n, device):
-        return remote(gat.at[ar, s, zz], gat.at[ar, s, zz], g_ssem.at[ar, n], g_rsem.at[ar, s, zz], device)
-
-    def share(ar, block):
-        gat[ar, sp, z] = block
-        sends = [gathered(ar, sp, z, n, {'tp': zpeer[k]}) for n, k in enumerate(SEND_ORDER)]
-        for copy in sends:
-            copy.start()
-
-        def pass_on(zz, n):
-            out = [gathered(ar, sp, zz, n + i, {'sp': peer}) for i, peer in enumerate((across, across_other, partner))]
-            for copy in out:
-                copy.start()
-            return out
-
-        sends += pass_on(z, 3)
-        for i, peer in enumerate(nearest):
-            gathered(ar, sp, peer, 0, {'tp': peer}).wait_recv()
-            sends += pass_on(peer, 6 + 3 * i)
-        for k in (0, 1, 2, 3):
-            for peer in (partner, across, across_other):
-                gathered(ar, peer, zpeer[k], 0, {'sp': peer}).wait_recv()
-        return sends
-
-    row0 = core * HALF_ROWS
-    col0 = yy * 2048 + z * 512
-    my_rows = dyn(row0, HALF_ROWS)
-    my_cols = dyn(col0, 512)
-
+    def scatter(ar, n):
+        return remote(rs_send.at[ar, n], rs_recv.at[ar, step[n] - 1], rs_ssem.at[ar, n],
+                      rs_rsem.at[ar, step[n] - 1], {'tp': target[n]})
+
+    def in_plane(c, zz, n, device):
+        return remote(gat.at[c, zz], gat.at[c, zz], g_ssem.at[n], g_rsem.at[c, zz], device)
+
+    def in_group(s, zz, n, device):
+        return remote(gat2.at[s, zz], gat2.at[s, zz], g2_ssem.at[n], g2_rsem.at[s, zz], device)
+
+    my_rows = dyn(yy * HALF_ROWS, HALF_ROWS)
+    my_cols = dyn(core * 2048 + z * 512, 512)
+
+    for load in wo_loads:
+        load.wait()
+    pending = []
+    for n in range(3):
+        rs_send[0, n] = jnp.dot(a_bf[...], wo_buf[target[n]], preferred_element_type=F32)
+        copy = scatter(0, n)
+        copy.start()
+        pending.append(copy)
+    begin(w1_loads[2:])
+    total = jnp.dot(a_bf[...], wo_buf[z], preferred_element_type=F32)
+    resid = hid_ref[my_rows, my_cols].astype(F32) + rows_ref[0, :, my_cols] + total
+
+    for copy in pending[:3]:
+        copy.wait_recv()
+    resid = (resid + (rs_recv[0, 0] + rs_recv[0, 1] + rs_recv[0, 2])).astype(BF16).astype(F32)
+
+    gat[core, z] = resid
+    sends = [in_plane(core, z, n, {'tp': target[n]}) for n in range(3)] + [in_plane(core, z, 3, {'sp': partner})]
+    for copy in sends:
+        copy.start()
+    begin(w2_loads[:2])
+    for i, peer in enumerate(nearest):
+        in_plane(core, peer, 0, {'tp': peer}).wait_recv()
+        copy = in_plane(core, peer, 4 + i, {'sp': partner})
+        copy.start()
+        sends.append(copy)
+    for zz in (z, *nearest):
+        in_plane(1 - core, zz, 0, {'sp': partner}).wait_recv()
+    pending += sends
+
+    begin(w2_loads[2:])
+    slots = [(c, zz) for c in range(2) for zz in range(4)]
+    acc = None
+    for c, zz in slots:
+        acc = gat[c, zz] if acc is None else acc + gat[c, zz]
+    mean = jnp.sum(acc, -1, keepdims=True) * (1.0 / DIM)
+    acc = None
+    for c, zz in slots:
+        centered = gat[c, zz] - mean
+        acc = centered * centered if acc is None else acc + centered * centered
+    scale = lax.rsqrt(jnp.sum(acc, -1, keepdims=True) * (1.0 / DIM) + LN_EPS)
+    for c, zz in slots:
+        cols = pl.ds(c * 2048 + zz * 512, 512)
+        y_bf[:, cols] = ((gat[c, zz] - mean) * scale * rows_ref[1, :, cols] + rows_ref[2, :, cols]).astype(BF16)
+
+    swaps = []
     for j in range(4):
-        loads[j].wait()
-    pending = []
-    for n, k in enumerate(SEND_ORDER):
-        rs_send[0, n] = jnp.dot(a_bf[...], wo_buf[zpeer[k]], preferred_element_type=F32)
-        copy = scatter(0, n, k)
-        copy.start()
-        pending.append(copy)
-    for load in loads[6:8]:
-        load.start(priority=1)
-    total = jnp.dot(a_bf[...], wo_buf[z], preferred_element_type=F32)
-
-    for copy in pending:
-        copy.wait_recv()
-    total = total + rs_recv[0, 0] + rs_recv[0, 1] + rs_recv[0, 2]
-    resid = (hid_ref[my_rows, my_cols].astype(F32) + total + rows_ref[0, :, my_cols]).astype(BF16).astype(F32)
-
-    pending += share(0, resid)
-
-    for load in loads[8:]:
-        load.start(priority=1)
-    for c in range(2):
-        slots = [(2 * y + c, zz) for y in range(2) for zz in range(4)]
-        acc = None
-        for s, zz in slots:
-            acc = gat[0, s, zz] if acc is None else acc + gat[0, s, zz]
-        mean = jnp.sum(acc, -1, keepdims=True) * (1.0 / DIM)
-        acc = None
-        for s, zz in slots:
-            centered = gat[0, s, zz] - mean
-            acc = centered * centered if acc is None else acc + centered * centered
-        scale = lax.rsqrt(jnp.sum(acc, -1, keepdims=True) * (1.0 / DIM) + LN_EPS)
-        for s, zz in slots:
-            cols = pl.ds((s // 2) * 2048 + zz * 512, 512)
-            y_bf[c * 16:(c + 1) * 16, cols] = ((gat[0, s, zz] - mean) * scale * rows_ref[1, :, cols]
-                                               + rows_ref[2, :, cols]).astype(BF16)
-
-    for j in range(4):
-        loads[4 + j].wait()
+        w1_loads[j].wait()
         part = jnp.dot(y_bf[...], w1_buf[j], preferred_element_type=F32)
         part = part + rows_ref[3, :, dyn(core * 2048 + j * 512, 512)]
-        u_bf[:, j * 512:(j + 1) * 512] = jnp.maximum(part, 0.0).astype(BF16)
-
+        act = jnp.maximum(part, 0.0).astype(BF16)
+        u_bf[:, j * 512:(j + 1) * 512] = act
+        u_send[j] = act.astype(F32)
+        copy = remote(u_send.at[j], u_recv.at[j], m_ssem.at[j], m_rsem.at[j], {'sp': partner})
+        copy.start()
+        swaps.append(copy)
+
+    own = []
+    for n in range(4):
+        w2_loads[n].wait()
+        own.append(jnp.dot(u_bf[...], w2_buf[0, n], preferred_element_type=F32))
     for j in range(4):
-        loads[8 + j].wait()
-    swaps = []
+        swaps[j].wait_recv()
+        x_bf[:, j * 512:(j + 1) * 512] = u_recv[j].astype(BF16)
     scatters = []
-
-    def merge(n):
-        swaps[n].wait_recv()
-        merged = m_own[n] + m_recv[n]
+    for n in range(4):
+        w2_loads[4 + n].wait()
+        total = own[n] + jnp.dot(x_bf[...], w2_buf[1, n], preferred_element_type=F32)
         if n < 3:
-            rs_send[1, n] = merged
-            copy = scatter(1, n, SEND_ORDER[n])
+            rs_send[1, n] = total
+            copy = scatter(1, n)
             copy.start()
             scatters.append(copy)
-        return merged
-
-    for n, k in enumerate(SEND_ORDER + (0,)):
-        part = jnp.dot(u_bf[...], w2_buf[zpeer[k]], preferred_element_type=F32)
-        m_send[n] = jnp.where(core == 0, part[16:], part[:16])
-        m_own[n] = jnp.where(core == 0, part[:16], part[16:])
-        copy = remote(m_send.at[n], m_recv.at[n], m_ssem.at[n], m_rsem.at[n], {'sp': partner})
-        copy.start()
-        swaps.append(copy)
-        if n >= 2:
-            merge(n - 2)
-    merge(2)
-    total = merge(3)
+    final = resid + rows_ref[4, :, my_cols] + total
 
     for copy in scatters:
         copy.wait_recv()
-    total = total + rs_recv[1, 0] + rs_recv[1, 1] + rs_recv[1, 2]
-    final = (resid + total + rows_ref[4, :, my_cols]).astype(BF16).astype(F32)
-
-    pending += share(1, final)
+    final = (final + (rs_recv[1, 0] + rs_recv[1, 1] + rs_recv[1, 2])).astype(BF16).astype(F32)
+
+    gat2[sp, z] = final
+    sends = [in_group(sp, z, n, {'tp': target[n]}) for n in range(3)]
+    for copy in sends:
+        copy.start()
+
+    def pass_on(zz, n):
+        out = [in_group(sp, zz, n + i, {'sp': peer}) for i, peer in enumerate((across, across_other, partner))]
+        for copy in out:
+            copy.start()
+        return out
+
+    sends += pass_on(z, 3)
+    for i, peer in enumerate(nearest):
+        in_group(sp, peer, 0, {'tp': peer}).wait_recv()
+        sends += pass_on(peer, 6 + 3 * i)
+    for zz in (z, *nearest):
+        for peer in (partner, across, across_other):
+            in_group(peer, zz, 0, {'sp': peer}).wait_recv()
+    pending += sends
 
     for s in range(4):
         for zz in range(4):
-            out_ref[(s % 2) * 16:(s % 2) * 16 + 16, (s // 2) * 2048 + zz * 512:(s // 2) * 2048 + zz * 512 + 512] = (
-                gat[1, s, zz].astype(BF16))
+            start = (s % 2) * 2048 + zz * 512
+            out_ref[(s // 2) * 16:(s // 2) * 16 + 16, start:start + 512] = gat2[s, zz].astype(BF16)
 
     for copy in (*c1, *c2, *pending, *swaps, *scatters):
         copy.wait_send()
@@ -453,21 +468,21 @@
             dma((6,)),
             pltpu.VMEM((4, 1024, 512), BF16),
             pltpu.VMEM((4, DIM, 512), BF16),
-            pltpu.VMEM((4, 2048, 512), BF16),
+            pltpu.VMEM((2, 4, 2048, 512), BF16),
             pltpu.VMEM((16, 8, 128), F32), pltpu.VMEM((2, 8, 128), F32),
             pltpu.VMEM((16, 8, 128), F32), pltpu.VMEM((2, 8, 128), F32),
             pltpu.VMEM((16, 8, 128), F32), pltpu.VMEM((2, 8, 128), F32),
             pltpu.VMEM((16, 8, 128), F32),
             pltpu.VMEM((16, 1024), BF16),
             pltpu.VMEM((2, 3, 16, 512), F32), pltpu.VMEM((2, 3, 16, 512), F32),
-            pltpu.VMEM((4, 16, 512), F32), pltpu.VMEM((4, 16, 512), F32), pltpu.VMEM((4, 16, 512), F32),
-            pltpu.VMEM((2, 4, 4, 16, 512), F32),
-            pltpu.VMEM((ROWS, DIM), BF16),
-            pltpu.VMEM((ROWS, 2048), BF16),
-            dma((4,)), dma((4,)), dma((4,)), dma((4,)), dma((4,)), dma((2, 3)), dma((2, 3)),
-            dma((4,)), dma((4,)), dma((2, 15)), dma((2, 4, 4)),
+            pltpu.VMEM((4, 16, 512), F32), pltpu.VMEM((4, 16, 512), F32),
+            pltpu.VMEM((2, 4, 16, 512), F32), pltpu.VMEM((4, 4, 16, 512), F32),
+            pltpu.VMEM((16, DIM), BF16),
+            pltpu.VMEM((16, 2048), BF16), pltpu.VMEM((16, 2048), BF16),
+            dma((4,)), dma((4,)), dma((2, 4)), dma((4,)), dma((4,)), dma((2, 3)), dma((2, 3)),
+            dma((4,)), dma((4,)), dma((7,)), dma((2, 4)), dma((15,)), dma((4, 4)),
         ],
-        compiler_params=pltpu.CompilerParams(collective_id=1, has_side_effects=True, vmem_limit_bytes=44 * MIB),
+        compiler_params=pltpu.CompilerParams(collective_id=1, has_side_effects=True, vmem_limit_bytes=48 * MIB),
         name='finish',
     )(o_part, stats, hidden, b_out, gain, bias, b_fc1, b_fc2, w_out, w_fc1, w_fc2)
 

time: 61.6 us -> 56.2 us (0.912)
  Pallas kernels: 60.2 us -> 54.7 us
    pallas_call x1, Pallas kernels: 42.9 us -> 38.3 us  [finish_call(): pl.pallas_call(finish_kernel, out_shape=jax.ShapeDtypeStruct((ROWS, DIM),...]
    pallas_call x1, Pallas kernels: 8.75 us -> 7.76 us  [qkv_call(): pl.pallas_call(qkv_kernel, out_shape=(jax.ShapeDtypeStruct((3, HEADS, ROW...]
where the time goes in v3:
time: 56.2 us; the launch traced here: 56.1 us
  Pallas kernels  54.7 us (97%)
  local copies, waits for them, and re-layouts  0.71 us (1%)
  between operations  0.67 us (1%)
    pallas_call x1, Pallas kernels, finish_call(): pl.pallas_call(finish_kernel, out_shape=jax.ShapeDtypeStruct((ROWS, DIM),...  38.3 us
    pallas_call x1, Pallas kernels, attn_call(): pl.pallas_call(attn_kernel, out_shape=(cache, cache, jax.ShapeDtypeStruct...  8.6 us
    pallas_call x1, Pallas kernels, qkv_call(): pl.pallas_call(qkv_kernel, out_shape=(jax.ShapeDtypeStruct((3, HEADS, ROW...  7.76 us

profile of v3, /device:TPU:0, one launch (start us, length us, event | category | flops | bytes accessed | tf_op | source)
XLA Modules:
  0.0 56.1 jit_solution(453943289813282491)
XLA Ops:
  0.6 0.0 copy-start
  0.6 7.8 %qkv.1 = (f32[3,8,32,128]{3,2,1,0:T(8,128)S(1)}, bf16[32,8,128,128]{3,2,1,0:T(8,128)(2,1)S(1)}) custom-call(bf16[32,4096]{1,0:T(8,128)(2,1)} %hid_hbm.1, bf16[4096]{0:T(1024)(128)(2,1)} %g_hbm.2, bf16[4096]{0:T(1024)(128)(2,1)} %b_hbm.2, bf16[4096,1024]{1,0:T(8,128)(2,1)} %wq_ref.1, bf16[4096,1024]{1,0:T(8,128)(2,1)} %wk_ref.1, bf16[4096,1024]{1,0:T(8,128)(2,1)} %wv_ref.1, ...), custom_call_target="tpu_custom_call" | custom-call | tf_op jit(solution)/shard_map/qkv/pallas_call | solution.py:112
  8.4 0.0 copy-done
  8.4 8.6 %attn.1 = (bf16[32,8,128,128]{3,2,1,0:T(8,128)(2,1)}, bf16[32,8,128,128]{3,2,1,0:T(8,128)(2,1)}, f32[32,8,128]{2,1,0:T(8,128)S(1)}, f32[2,8,128]{2,1,0:T(8,128)S(1)}, bf16[32,8,128,128]{3,2,1,0:T(8,128)(2,1)S(1)}) custom-call(s32[32]{0:T(128)S(1)} %copy-done, f32[3,8,32,128]{3,2,1,0:T(8,128)S(1)} %get-tuple-element.9.qkv_ref, ...), custom_call_target="tpu_custom_call", output_to_operand_aliasing={{4}: (2, {})} | custom-call | tf_op jit(solution)/shard_map/attn/pallas_call | solution.py:228
  17.0 38.3 %finish.1 = bf16[32,4096]{1,0:T(8,128)(2,1)S(1)} custom-call(f32[32,8,128]{2,1,0:T(8,128)S(1)} %get-tuple-element.11.o_ref, f32[2,8,128]{2,1,0:T(8,128)S(1)} %get-tuple-element.12.st_ref, bf16[32,4096]{1,0:T(8,128)(2,1)} %hid_hbm.1, bf16[4096]{0:T(1024)(128)(2,1)} %bo_hbm.1, bf16[4096]{0:T(1024)(128)(2,1)} %g_hbm.3, bf16[4096]{0:T(1024)(128)(2,1)} %b_hbm.3, ...), custom_call_target="tpu_custom_call" | custom-call | tf_op jit(solution)/shard_map/finish/pallas_call | solution.py:459
  55.3 0.7 %copy.26 = bf16[32,4096]{1,0:T(8,128)(2,1)} copy(bf16[32,4096]{1,0:T(8,128)(2,1)S(1)} %finish.1) | data formatting | bytes 524288
Async XLA Ops:
  0.6 7.8 %copy-start = (s32[32]{0:T(128)S(1)}, s32[32]{0:T(128)}, u32[]{:S(2)}) copy-start(s32[32]{0:T(128)} %pos_ref.1) | copy-start | bytes 388

commit v4 on v3

--- a/solution.py
+++ b/solution.py
@@ -136,8 +136,10 @@
 CHUNK = 4
 NUM_CHUNKS = ROWS // CHUNK
 
-def attn_kernel(pos_ref, qkv_ref, k_in, v_hbm, k_out, v_out, o_ref, st_ref, kbuf, vbuf, qs, vin, kdone, vdone):
+def attn_kernel(pos_hbm, qkv_ref, k_in, v_hbm, k_out, v_out, o_ref, st_ref, kbuf, vbuf, qs, pos_ref, pos_sem, vin, kdone, vdone):
     base = lax.axis_index('sp') * BLOCK_LEN
+    pos_copy = pltpu.make_async_copy(pos_hbm, pos_ref, pos_sem)
+    pos_copy.start()
 
     def chunk_copy(src, dst, sem, p):
         rows = pl.ds(p * CHUNK, CHUNK)
@@ -148,6 +150,7 @@
 
     for i in range(3):
         qs[i] = jnp.swapaxes(qkv_ref[i], 0, 1)
+    pos_copy.wait()
 
     row = lax.broadcasted_iota(jnp.int32, (16, 128), 0)
     lane = lax.broadcasted_iota(jnp.int32, (16, 128), 1)
@@ -229,12 +232,14 @@
         attn_kernel,
         out_shape=(cache, cache, jax.ShapeDtypeStruct((ROWS, HEADS, HEAD_DIM), F32),
                    jax.ShapeDtypeStruct((2, HEADS, 128), F32), pltpu.VMEM(k_cache.shape, BF16)),
-        in_specs=[pl.BlockSpec(memory_space=pltpu.SMEM), vmem_spec(), vmem_spec(), any_spec()],
+        in_specs=[any_spec(), vmem_spec(), vmem_spec(), any_spec()],
         out_specs=(any_spec(), any_spec(), vmem_spec(), vmem_spec(), vmem_spec()),
         input_output_aliases={2: 4},
         scratch_shapes=[
             pltpu.VMEM(k_cache.shape, BF16),
             pltpu.VMEM((3, ROWS, HEADS, HEAD_DIM), F32),
+            pltpu.SMEM((ROWS,), jnp.int32),
+            pltpu.SemaphoreType.DMA,
             pltpu.SemaphoreType.DMA((NUM_CHUNKS,)),
             pltpu.SemaphoreType.DMA((NUM_CHUNKS,)),
             pltpu.SemaphoreType.DMA((NUM_CHUNKS,)),
@@ -431,19 +436,31 @@
     for copy in sends:
         copy.start()
 
-    def pass_on(zz, n):
-        out = [in_group(sp, zz, n + i, {'sp': peer}) for i, peer in enumerate((across, across_other, partner))]
+    def pass_on(slot, zz, n, peers):
+        out = [in_group(slot, zz, n + i, {'sp': peer}) for i, peer in enumerate(peers)]
         for copy in out:
             copy.start()
         return out
 
-    sends += pass_on(z, 3)
+    def hand_on(zz, n):
+        in_group(across, zz, 0, {'sp': across}).wait_recv()
+        return pass_on(across, zz, n, (partner,))
+
+    sends += pass_on(sp, z, 3, (across, partner))
     for i, peer in enumerate(nearest):
         in_group(sp, peer, 0, {'tp': peer}).wait_recv()
-        sends += pass_on(peer, 6 + 3 * i)
+        if i < 2:
+            sends += pass_on(sp, peer, 5 + 2 * i, (across, partner))
+        else:
+            sends += pass_on(sp, peer, 9, (across, across_other, partner))
+        if i == 1:
+            sends += hand_on(z, 12)
+    for i in range(2):
+        sends += hand_on(nearest[i], 13 + i)
     for zz in (z, *nearest):
-        for peer in (partner, across, across_other):
-            in_group(peer, zz, 0, {'sp': peer}).wait_recv()
+        in_group(partner, zz, 0, {'sp': partner}).wait_recv()
+        in_group(across_other, zz, 0, {'sp': across_other}).wait_recv()
+    in_group(across, nearest[2], 0, {'sp': across}).wait_recv()
     pending += sends
 
     for s in range(4):
@@ -497,7 +514,7 @@
     def local_layer(hidden, positions, k_cache, v_cache, ln1_gain, ln1_bias, w_query, b_query, w_key, b_key, w_value, b_value, w_out, b_out, ln2_gain, ln2_bias, w_fc1, b_fc1, w_fc2, b_fc2):
         keep = lambda array: pltpu.with_memory_space_constraint(array, pltpu.HBM)
         qkv, k_vmem = qkv_call(*map(keep, (hidden, ln1_gain, ln1_bias, w_query, b_query, w_key, b_key, w_value, b_value, k_cache)))
-        k_next, v_next, o_part, stats, _ = attn_call(positions, qkv, k_vmem, keep(v_cache))
+        k_next, v_next, o_part, stats, _ = attn_call(keep(positions), qkv, k_vmem, keep(v_cache))
         result = finish_call(o_part, stats, *map(keep, (hidden, b_out, ln2_gain, ln2_bias, b_fc1, b_fc2, w_out, w_fc1, w_fc2)))
         return result, k_next, v_next
 

time: 56.2 us -> 55.8 us (level)
  no operation moved by 1% of the time
where the time goes in v4:
time: 55.8 us; the launch traced here: 55.6 us
  Pallas kernels  54.2 us (97%)
  local copies, waits for them, and re-layouts  0.71 us (1%)
  between operations  0.66 us (1%)
    pallas_call x1, Pallas kernels, finish_call(): pl.pallas_call(finish_kernel, out_shape=jax.ShapeDtypeStruct((ROWS, DIM),...  38.4 us
    pallas_call x1, Pallas kernels, attn_call(): pl.pallas_call(attn_kernel, out_shape=(cache, cache, jax.ShapeDtypeStruct...  8.07 us
    pallas_call x1, Pallas kernels, qkv_call(): pl.pallas_call(qkv_kernel, out_shape=(jax.ShapeDtypeStruct((3, HEADS, ROW...  7.76 us

profile of v4, /device:TPU:0, one launch (start us, length us, event | category | flops | bytes accessed | tf_op | source)
XLA Modules:
  0.0 55.6 jit_solution(1470581134848047621)
XLA Ops:
  0.6 7.8 %qkv.1 = (f32[3,8,32,128]{3,2,1,0:T(8,128)S(1)}, bf16[32,8,128,128]{3,2,1,0:T(8,128)(2,1)S(1)}) custom-call(bf16[32,4096]{1,0:T(8,128)(2,1)} %hid_hbm.1, bf16[4096]{0:T(1024)(128)(2,1)} %g_hbm.2, bf16[4096]{0:T(1024)(128)(2,1)} %b_hbm.2, bf16[4096,1024]{1,0:T(8,128)(2,1)} %wq_ref.1, bf16[4096,1024]{1,0:T(8,128)(2,1)} %wk_ref.1, bf16[4096,1024]{1,0:T(8,128)(2,1)} %wv_ref.1, ...), custom_call_target="tpu_custom_call" | custom-call | tf_op jit(solution)/shard_map/qkv/pallas_call | solution.py:112
  8.4 8.1 %attn.1 = (bf16[32,8,128,128]{3,2,1,0:T(8,128)(2,1)}, bf16[32,8,128,128]{3,2,1,0:T(8,128)(2,1)}, f32[32,8,128]{2,1,0:T(8,128)S(1)}, f32[2,8,128]{2,1,0:T(8,128)S(1)}, bf16[32,8,128,128]{3,2,1,0:T(8,128)(2,1)S(1)}) custom-call(s32[32]{0:T(128)} %pos_hbm.1, f32[3,8,32,128]{3,2,1,0:T(8,128)S(1)} %get-tuple-element.9.qkv_ref, ...), custom_call_target="tpu_custom_call", output_to_operand_aliasing={{4}: (2, {})} | custom-call | tf_op jit(solution)/shard_map/attn/pallas_call | solution.py:231
  16.5 38.4 %finish.1 = bf16[32,4096]{1,0:T(8,128)(2,1)S(1)} custom-call(f32[32,8,128]{2,1,0:T(8,128)S(1)} %get-tuple-element.11.o_ref, f32[2,8,128]{2,1,0:T(8,128)S(1)} %get-tuple-element.12.st_ref, bf16[32,4096]{1,0:T(8,128)(2,1)} %hid_hbm.1, bf16[4096]{0:T(1024)(128)(2,1)} %bo_hbm.1, bf16[4096]{0:T(1024)(128)(2,1)} %g_hbm.3, bf16[4096]{0:T(1024)(128)(2,1)} %b_hbm.3, ...), custom_call_target="tpu_custom_call" | custom-call | tf_op jit(solution)/shard_map/finish/pallas_call | solution.py:476
  54.9 0.7 %copy.26 = bf16[32,4096]{1,0:T(8,128)(2,1)} copy(bf16[32,4096]{1,0:T(8,128)(2,1)S(1)} %finish.1) | data formatting | bytes 524288

commit v5 on v4

--- a/solution.py
+++ b/solution.py
@@ -372,7 +372,7 @@
     sends = [in_plane(core, z, n, {'tp': target[n]}) for n in range(3)] + [in_plane(core, z, 3, {'sp': partner})]
     for copy in sends:
         copy.start()
-    begin(w2_loads[:2])
+    begin(w2_loads[:4])
     for i, peer in enumerate(nearest):
         in_plane(core, peer, 0, {'tp': peer}).wait_recv()
         copy = in_plane(core, peer, 4 + i, {'sp': partner})
@@ -382,7 +382,7 @@
         in_plane(1 - core, zz, 0, {'sp': partner}).wait_recv()
     pending += sends
 
-    begin(w2_loads[2:])
+    begin(w2_loads[4:])
     slots = [(c, zz) for c in range(2) for zz in range(4)]
     acc = None
     for c, zz in slots:

time: 55.8 us -> 55.8 us (level)
  no operation moved by 1% of the time
where the time goes in v5:
time: 55.8 us; the launch traced here: 55.7 us
  Pallas kernels  54.3 us (97%)
  local copies, waits for them, and re-layouts  0.71 us (1%)
  between operations  0.66 us (1%)
    pallas_call x1, Pallas kernels, finish_call(): pl.pallas_call(finish_kernel, out_shape=jax.ShapeDtypeStruct((ROWS, DIM),...  38.5 us
    pallas_call x1, Pallas kernels, attn_call(): pl.pallas_call(attn_kernel, out_shape=(cache, cache, jax.ShapeDtypeStruct...  8.12 us
    pallas_call x1, Pallas kernels, qkv_call(): pl.pallas_call(qkv_kernel, out_shape=(jax.ShapeDtypeStruct((3, HEADS, ROW...  7.76 us

profile of v5, /device:TPU:0, one launch (start us, length us, event | category | flops | bytes accessed | tf_op | source)
XLA Modules:
  0.0 55.7 jit_solution(9780445353476868096)
XLA Ops:
  0.6 7.8 %qkv.1 = (f32[3,8,32,128]{3,2,1,0:T(8,128)S(1)}, bf16[32,8,128,128]{3,2,1,0:T(8,128)(2,1)S(1)}) custom-call(bf16[32,4096]{1,0:T(8,128)(2,1)} %hid_hbm.1, bf16[4096]{0:T(1024)(128)(2,1)} %g_hbm.2, bf16[4096]{0:T(1024)(128)(2,1)} %b_hbm.2, bf16[4096,1024]{1,0:T(8,128)(2,1)} %wq_ref.1, bf16[4096,1024]{1,0:T(8,128)(2,1)} %wk_ref.1, bf16[4096,1024]{1,0:T(8,128)(2,1)} %wv_ref.1, ...), custom_call_target="tpu_custom_call" | custom-call | tf_op jit(solution)/shard_map/qkv/pallas_call | solution.py:112
  8.4 8.1 %attn.1 = (bf16[32,8,128,128]{3,2,1,0:T(8,128)(2,1)}, bf16[32,8,128,128]{3,2,1,0:T(8,128)(2,1)}, f32[32,8,128]{2,1,0:T(8,128)S(1)}, f32[2,8,128]{2,1,0:T(8,128)S(1)}, bf16[32,8,128,128]{3,2,1,0:T(8,128)(2,1)S(1)}) custom-call(s32[32]{0:T(128)} %pos_hbm.1, f32[3,8,32,128]{3,2,1,0:T(8,128)S(1)} %get-tuple-element.9.qkv_ref, ...), custom_call_target="tpu_custom_call", output_to_operand_aliasing={{4}: (2, {})} | custom-call | tf_op jit(solution)/shard_map/attn/pallas_call | solution.py:231
  16.5 38.5 %finish.1 = bf16[32,4096]{1,0:T(8,128)(2,1)S(1)} custom-call(f32[32,8,128]{2,1,0:T(8,128)S(1)} %get-tuple-element.11.o_ref, f32[2,8,128]{2,1,0:T(8,128)S(1)} %get-tuple-element.12.st_ref, bf16[32,4096]{1,0:T(8,128)(2,1)} %hid_hbm.1, bf16[4096]{0:T(1024)(128)(2,1)} %bo_hbm.1, bf16[4096]{0:T(1024)(128)(2,1)} %g_hbm.3, bf16[4096]{0:T(1024)(128)(2,1)} %b_hbm.3, ...), custom_call_target="tpu_custom_call" | custom-call | tf_op jit(solution)/shard_map/finish/pallas_call | solution.py:476
  55.0 0.7 %copy.26 = bf16[32,4096]{1,0:T(8,128)(2,1)} copy(bf16[32,4096]{1,0:T(8,128)(2,1)S(1)} %finish.1) | data formatting | bytes 524288
